TPU v7x, 32 devices: a whole 2x2x4 slice. The times are simulated.
32 devices in a mesh: tm: 8 (over z, core), block: 4 (over y, x).
Axes of the slice: x: 2, y: 2, z: 4, core: 2. Of those that a mesh axis runs over, the one named last changes fastest.
Arguments:
- state: float32 [16, 4, 256, 512], P('tm', None, None, 'block'), may hold values from -6 to 6
- far_field: float32 [16, 4, 512], P('tm', None, 'block'), may hold values from -6 to 6
- face_index: int32 [16, 512], P('tm', 'block'), may hold values from 0 to 255, as said below
- face_weight: float32 [16, 4, 512], P('tm', None, 'block'), may hold values from 0.05 to 0.45
- mean_flow: float32 [2, 2], replicated, may hold values from -0.6 to 0.6
Outputs:
- new_state: float32 [16, 4, 256, 512], P('tm', None, None, 'block')
Inputs may be any that keep to these rules, and one draw needn't show every extreme that they name: `face_index`: each face's index points into the opposite row's 2 * 128 interface faces laid end to end; the 4 faces read wrap around that cycle. At each level, the faces of one blade row take distinct first indices, every face of the opposite row exactly once.
All inputs are finite; a program needn't handle non-finite values.
Results may differ from a plain program's by a relative error of at most 0.00016.
Values sent between devices are 32-bit elements; how exact they have to be, the bound alone decides.
A program may use at most 64 MiB of HBM per device.

v0:
```python
import functools
import math

import jax
import jax.numpy as jnp
from jax import lax
from jax.experimental import pallas as pl
from jax.experimental.pallas import tpu as pltpu
from jax.sharding import PartitionSpec as P

SECTION_FACTORS = (0.075, 0.05, 0.1125, 0.15, 0.3)
OMEGA = 1.0
DISSIPATION = 0.2
PAD = 8
MESH = pl.DeviceIdType.MESH


def split_coefficients(count, scale):
    half = count // 2
    d = [0.0] + [0.5 * (-1) ** k / math.tan(math.pi * k / count) for k in range(1, half)] + [0.0]
    even = [0.5 * scale * (d[m] - d[half - m]) for m in range(half)]
    odd = [0.5 * scale * (d[m] + d[half - m]) for m in range(half)]
    even[0] = odd[0] = 0.0
    return even, odd


def time_term(q, even, odd):
    half = len(q) // 2
    quarter = half // 2
    e = [q[n] + q[n + half] for n in range(half)]
    o = [q[n] - q[n + half] for n in range(half)]

    def odd_at(n):
        return (o[n % half], -1.0 if (n // half) % 2 else 1.0)

    low, high = [], []
    for n in range(half):
        ev = None
        od = None
        for m in range(1, quarter):
            term = even[m] * (e[(n - m) % half] - e[(n + m) % half])
            ev = term if ev is None else ev + term
            (a, sa), (b, sb) = odd_at(n - m), odd_at(n + m)
            pair = a - b if sa == sb else a + b
            term = (odd[m] * sa) * pair
            od = term if od is None else od + term
        a, sa = odd_at(n - quarter)
        od = od + (odd[quarter] * sa) * a
        low.append(ev + od)
        high.append(ev - od)
    return low + high


def kernel(dims, state, far, fidx, fw, mf, out, x0, qa, qb, ef, el, rl, ru, cs, cl, cu,
           face, ff, wts, fi, lane_ix, blk_ix, ww, gh,
           in_s, in_r, out_s, out_r, p_s, p_r, h_s, h_r, f_s, f_r, loc):
    tm_n, half, L, R, K = dims
    NT = tm_n * L
    cycle = half * 128
    tiles = R // 8
    nsec = len(SECTION_FACTORS)
    me = lax.axis_index("tm")
    blk = lax.axis_index("block")
    side = lax.div(blk, half)
    place = lax.rem(blk, half)
    row0 = side * half
    lower_b = row0 + lax.rem(place + half - 1, half)
    upper_b = row0 + lax.rem(place + 1, half)
    other0 = (1 - side) * half
    step = 1 - 2 * side
    is_last = me == tm_n - 1
    is_far = me == 0
    rchunk = side * (tm_n - 1) + step * me
    has_lower = rchunk > 0
    has_upper = rchunk < tm_n - 1
    ghost_row = jnp.where(side == 0, PAD + R, PAD - 1)
    far_row = jnp.where(side == 0, PAD - 1, PAD + R)

    def rc(src, dst, ss, rs, dev):
        return pltpu.make_async_remote_copy(src_ref=src, dst_ref=dst, send_sem=ss, recv_sem=rs,
                                            device_id=dev, device_id_type=MESH)

    def rows(p):
        return pl.ds(pl.multiple_of((side * (tm_n - 1) + step * p) * R, R), R)

    def lev(p):
        return pl.ds(p * L, L)

    def peer(t):
        return lax.rem(me + 1 + t, tm_n)

    bar = pltpu.get_barrier_semaphore()

    @pl.loop(0, tm_n - 1)
    def _(t):
        pl.semaphore_signal(bar, inc=1, device_id={"tm": peer(t)}, device_id_type=MESH)

    pl.semaphore_signal(bar, inc=1, device_id={"block": lower_b}, device_id_type=MESH)
    pl.semaphore_signal(bar, inc=1, device_id={"block": upper_b}, device_id_type=MESH)

    @pl.when(is_last)
    def _():
        for h in range(half):
            pl.semaphore_signal(bar, inc=1, device_id={"block": other0 + h}, device_id_type=MESH)

    own = pltpu.make_async_copy(state.at[:, :, rows(me)], x0.at[lev(me)], loc.at[0])
    own.start()
    pl.semaphore_wait(bar, tm_n + 1 + jnp.where(is_last, half, 0))

    def in_copy(p, src_tm):
        return rc(state.at[:, :, rows(p)], x0.at[lev(src_tm)], in_s.at[p], in_r.at[src_tm], {"tm": p})

    @pl.loop(0, tm_n - 1)
    def _(t):
        p = peer(t)
        in_copy(p, me).start()

    def far_copy(src_tm):
        return rc(far, ff.at[lev(src_tm)], p_s.at[0], p_r.at[0, src_tm], {"tm": 0})

    def wt_copy(src_tm):
        return rc(fw, wts.at[lev(src_tm)], p_s.at[1], p_r.at[1, src_tm], {"tm": tm_n - 1})

    def ix_copy(src_tm):
        return rc(fidx, fi.at[src_tm], p_s.at[2], p_r.at[2, src_tm], {"tm": tm_n - 1})

    own_far = pltpu.make_async_copy(far, ff.at[lev(me)], loc.at[1])
    own_wt = pltpu.make_async_copy(fw, wts.at[lev(me)], loc.at[2])
    own_ix = pltpu.make_async_copy(fidx, fi.at[me], loc.at[3])

    @pl.when(is_far)
    def _():
        own_far.start()

    @pl.when(jnp.logical_not(is_far))
    def _():
        far_copy(me).start()

    @pl.when(is_last)
    def _():
        own_wt.start()
        own_ix.start()

    @pl.when(jnp.logical_not(is_last))
    def _():
        wt_copy(me).start()
        ix_copy(me).start()

    lane = lax.broadcasted_iota(jnp.int32, (8, 128), 1)
    lane_pair = jnp.bitwise_or(lane, 1)
    sub = lax.broadcasted_iota(jnp.int32, (8, 128), 0)

    def pack(acc, value, k):
        return jnp.where(lane_pair == k, pltpu.roll(value, k, 1), acc)

    def key(l, v):
        return 2 * (4 * l + v) + 1

    def halo_copies(s):
        low = rc(ef.at[s], ru.at[s], h_s.at[s, 0], h_r.at[s, 0], {"tm": me - step})
        up = rc(el.at[s], rl.at[s], h_s.at[s, 1], h_r.at[s, 1], {"tm": me + step})
        jl = rc(cs.at[s], cu.at[s], h_s.at[s, 2], h_r.at[s, 2], {"block": lower_b})
        ju = rc(cs.at[s], cl.at[s], h_s.at[s, 3], h_r.at[s, 3], {"block": upper_b})
        return low, up, jl, ju

    def face_copy(s, h, edge):
        return rc(edge.at[s], face.at[s, place], f_s.at[s, h], f_r.at[s, place], {"block": other0 + h})

    def face_wait(s, h):
        return rc(ef.at[s], face.at[s, h], f_s.at[s, h], f_r.at[s, h], {"block": other0 + h})

    def send_halos(s):
        low, up, jl, ju = halo_copies(s)

        @pl.when(is_last & (side == 0))
        def _():
            for h in range(half):
                face_copy(s, h, el).start()

        @pl.when(is_last & (side == 1))
        def _():
            for h in range(half):
                face_copy(s, h, ef).start()

        @pl.when(has_lower)
        def _():
            low.start()

        @pl.when(has_upper)
        def _():
            up.start()

        jl.start()
        ju.start()

    def take_level(l, accs):
        accs = list(accs)
        for v in range(4):
            for a in range(tiles):
                value = x0[l, v, pl.ds(8 * a, 8)]
                qa[l, v, pl.ds(PAD + 8 * a, 8)] = value
                accs[a] = pack(accs[a], value, key(l, v))
                if a == 0:
                    ef[0, pl.ds(4 * l + v, 1)] = value[0:1]
                if a == tiles - 1:
                    el[0, pl.ds(4 * l + v, 1)] = value[7:8]
        return tuple(accs)

    own.wait()
    accs = tuple(jnp.zeros((8, 128), jnp.float32) for _ in range(tiles))
    accs = lax.fori_loop(0, L, lambda j, c: take_level(me * L + j, c), accs)

    def arrive(t, c):
        p = peer(tm_n - 2 - t)
        in_copy(p, p).wait_recv()
        return lax.fori_loop(0, L, lambda j, d: take_level(p * L + j, d), c)

    accs = lax.fori_loop(0, tm_n - 1, arrive, accs)
    for a in range(tiles):
        cs[0, pl.ds(8 * a, 8)] = accs[a]
    send_halos(0)

    @pl.when(is_far)
    def _():
        own_far.wait()

        @pl.loop(1, tm_n)
        def _(p):
            far_copy(p).wait_recv()

        @pl.loop(0, NT)
        def _(l):
            for v in range(4):
                row = ff[l, pl.ds(v, 1)]
                qa[l, v, pl.ds(far_row, 1)] = row
                qb[l, v, pl.ds(far_row, 1)] = row

    @pl.when(is_last)
    def _():
        own_wt.wait()
        own_ix.wait()

        @pl.loop(0, tm_n - 1)
        def _(p):
            wt_copy(p).wait_recv()
            ix_copy(p).wait_recv()

        @pl.loop(0, NT // 2)
        def _(m):
            def ix(l):
                return jnp.broadcast_to(fi[lax.div(l, L), pl.ds(lax.rem(l, L), 1)], (8, 128))

            def wt(l, k):
                return jnp.broadcast_to(wts[l, pl.ds(k, 1)], (8, 128))

            start = jnp.where(sub < 4, ix(2 * m), ix(2 * m + 1))
            at = pl.ds(8 * m, 8)
            for k in range(K):
                src = start + k
                src = jnp.where(src >= cycle, src - cycle, src)
                lane_ix[k, at] = jnp.bitwise_and(src, 127)
                blk_ix[k, at] = lax.shift_right_logical(src, 7)
                ww[k, at] = jnp.where(sub < 4, wt(2 * m, k), wt(2 * m + 1, k))

    speed_u = jnp.where(side == 0, mf[0, 0], mf[1, 0])
    speed_v = jnp.where(side == 0, mf[0, 1], mf[1, 1])
    odd_lane = jnp.bitwise_and(lane, 1) == 1
    edge_lane = {0: lane == 0, 127: lane == 127}

    def install(dst, src, at):
        @pl.loop(0, NT)
        def _(l):
            for v in range(4):
                dst[l, v, pl.ds(at, 1)] = src[pl.ds(4 * l + v, 1)]

    def out_copy(q, p, src_tm):
        return rc(q.at[lev(p), :, pl.ds(PAD, R)], out.at[:, :, rows(src_tm)],
                  out_s.at[p], out_r.at[src_tm], {"tm": p})

    for s, factor in enumerate(SECTION_FACTORS):
        q, nq = (qa, qb) if s % 2 == 0 else (qb, qa)
        final = s == nsec - 1
        even, odd = split_coefficients(NT, OMEGA * factor)
        hu, hv, hh = (0.5 * factor) * speed_u, (0.5 * factor) * speed_v, 0.5 * factor

        @pl.loop(0, 4)
        def _(v):
            @pl.loop(0, tiles)
            def _(a):
                at = pl.ds(pl.multiple_of(PAD + 8 * a, 8), 8)
                xs = [q[l, v, at] for l in range(NT)]
                terms = time_term(xs, even, odd)
                for l in range(NT):
                    first = x0[l, v, pl.ds(pl.multiple_of(8 * a, 8), 8)]
                    nq[l, v, at] = first - (terms[l] + (4.0 * DISSIPATION * factor) * xs[l])

        low, up, jl, ju = halo_copies(s)
        jl.wait_recv()
        ju.wait_recv()
        mixed = []
        for a in range(tiles):
            at = pl.ds(8 * a, 8)
            mixed.append(jnp.where(odd_lane, pltpu.roll(cl[s, at], 1, 1), pltpu.roll(cu[s, at], 127, 1)))

        def level(l, accs, which):
            accs = list(accs)
            for slot, a in enumerate(which):
                base = PAD + 8 * a
                di, dj, near = [], [], []
                for v in range(4):
                    x = q[l, v, pl.ds(base, 8)]
                    upx = q[l, v, pl.ds(base + 1, 8)]
                    dnx = q[l, v, pl.ds(base - 1, 8)]
                    border = pltpu.roll(mixed[a], 128 - key(l, v), 1)
                    left = jnp.where(edge_lane[0], border, pltpu.roll(x, 1, 1))
                    right = jnp.where(edge_lane[127], border, pltpu.roll(x, 127, 1))
                    di.append(upx - dnx)
                    dj.append(right - left)
                    near.append((DISSIPATION * factor) * ((upx + dnx) + (right + left)))
                flux = [
                    hu * di[0] + hv * dj[0] + hh * (di[1] + dj[2]),
                    hu * di[1] + hv * dj[1] + hh * di[3],
                    hu * di[2] + hv * dj[2] + hh * dj[3],
                    hu * di[3] + hv * dj[3] + hh * (di[1] + dj[2]),
                ]
                for v in range(4):
                    new = nq[l, v, pl.ds(base, 8)] + (near[v] - flux[v])
                    nq[l, v, pl.ds(base, 8)] = new
                    if not final:
                        accs[slot] = pack(accs[slot], new, key(l, v))
                        if a == 0:
                            ef[s + 1, pl.ds(4 * l + v, 1)] = new[0:1]
                        if a == tiles - 1:
                            el[s + 1, pl.ds(4 * l + v, 1)] = new[7:8]
            return tuple(accs)

        def sweep(which):
            zero = tuple(jnp.zeros((8, 128), jnp.float32) for _ in which)
            step_by = 4 if NT % 4 == 0 else 1

            def several(g, c):
                for j in range(step_by):
                    c = level(step_by * g + j, c, which)
                return c

            accs = lax.fori_loop(0, NT // step_by, several, zero)
            if not final:
                for slot, a in enumerate(which):
                    cs[s + 1, pl.ds(8 * a, 8)] = accs[slot]

        inner = tuple(range(1, tiles - 1))
        outer = tuple(sorted({0, tiles - 1}))
        if inner:
            sweep(inner)

        @pl.when(has_lower)
        def _():
            up.wait_recv()
            install(q, rl.at[s], PAD - 1)

        @pl.when(has_upper)
        def _():
            low.wait_recv()
            install(q, ru.at[s], PAD + R)

        @pl.when(is_last)
        def _():
            for h in range(half):
                face_wait(s, h).wait_recv()

            @pl.loop(0, NT // 2)
            def _(m):
                at = pl.ds(8 * m, 8)
                total = jnp.zeros((8, 128), jnp.float32)
                for k in range(K):
                    picked = jnp.zeros((8, 128), jnp.float32)
                    for h in range(half):
                        got = jnp.take_along_axis(face[s, h, at], lane_ix[k, at], axis=1)
                        picked = jnp.where(blk_ix[k, at] == h, got, picked)
                    total = total + ww[k, at] * picked
                gh[at] = total

            install(q, gh, ghost_row)

        if not final:
            sweep(outer)
            send_halos(s + 1)
        else:
            def finish(t, c):
                p = peer(t)
                for j in range(L):
                    level(p * L + j, (None,) * len(outer), outer)

                @pl.when(t < tm_n - 1)
                def _():
                    out_copy(nq, p, me).start()

                return c

            lax.fori_loop(0, tm_n, finish, 0)
            own_out = pltpu.make_async_copy(nq.at[lev(me), :, pl.ds(PAD, R)], out.at[:, :, rows(me)], loc.at[4])
            own_out.start()

            @pl.loop(0, tm_n - 1)
            def _(t):
                p = peer(t)
                out_copy(nq, p, p).wait_recv()

            own_out.wait()

            @pl.loop(0, tm_n - 1)
            def _(t):
                p = peer(t)
                out_copy(nq, p, me).wait_send()

    @pl.loop(0, tm_n - 1)
    def _(t):
        p = peer(t)
        in_copy(p, me).wait_send()

    @pl.when(jnp.logical_not(is_far))
    def _():
        far_copy(me).wait_send()

    @pl.when(jnp.logical_not(is_last))
    def _():
        wt_copy(me).wait_send()
        ix_copy(me).wait_send()

    for s in range(nsec):
        low, up, jl, ju = halo_copies(s)

        @pl.when(has_lower)
        def _():
            low.wait_send()

        @pl.when(has_upper)
        def _():
            up.wait_send()

        jl.wait_send()
        ju.wait_send()

        @pl.when(is_last)
        def _():
            for h in range(half):
                face_wait(s, h).wait_send()


def shards(dims, state, far_field, face_index, face_weight, mean_flow):
    tm_n, half = dims
    L, _, rows, width = state.shape
    K = face_weight.shape[1]
    R = rows // tm_n
    NT = L * tm_n
    assert width == 128 and NT % 4 == 0 and R % 8 == 0 and 8 * NT <= width
    n = len(SECTION_FACTORS)
    f32 = jnp.float32
    hbm = pl.BlockSpec(memory_space=pl.ANY)
    dma = pltpu.SemaphoreType.DMA
    V = pltpu.VMEM
    return pl.pallas_call(
        functools.partial(kernel, (tm_n, half, L, R, K)),
        out_shape=jax.ShapeDtypeStruct(state.shape, f32),
        in_specs=[hbm, hbm, hbm, hbm, pl.BlockSpec(memory_space=pltpu.SMEM)],
        out_specs=hbm,
        scratch_shapes=[
            V((NT, 4, R, width), f32),
            V((NT, 4, R + 2 * PAD, width), f32),
            V((NT, 4, R + 2 * PAD, width), f32),
            V((n, 4 * NT, width), f32),
            V((n, 4 * NT, width), f32),
            V((n, 4 * NT, width), f32),
            V((n, 4 * NT, width), f32),
            V((n, R, width), f32),
            V((n, R, width), f32),
            V((n, R, width), f32),
            V((n, half, 4 * NT, width), f32),
            V((NT, 4, width), f32),
            V((NT, K, width), f32),
            V((tm_n, L, width), jnp.int32),
            V((K, 4 * NT, width), jnp.int32),
            V((K, 4 * NT, width), jnp.int32),
            V((K, 4 * NT, width), f32),
            V((4 * NT, width), f32),
            dma((tm_n,)), dma((tm_n,)), dma((tm_n,)), dma((tm_n,)),
            dma((3,)), dma((3, tm_n)),
            dma((n, 4)), dma((n, 4)),
            dma((n, half)), dma((n, half)),
            dma((5,)),
        ],
        compiler_params=pltpu.CompilerParams(
            collective_id=0, has_side_effects=True, vmem_limit_bytes=40 * 1024 * 1024),
    )(state, far_field, face_index, face_weight, mean_flow)


def solution(mesh):
    dims = (mesh.shape["tm"], mesh.shape["block"] // 2)
    in_specs = (
        P("tm", None, None, "block"),
        P("tm", None, "block"),
        P("tm", "block"),
        P("tm", None, "block"),
        P(),
    )
    out_specs = P("tm", None, None, "block")
    return jax.shard_map(functools.partial(shards, dims), mesh=mesh, in_specs=in_specs,
                         out_specs=out_specs, check_vma=False)
```

profile of v0, /device:TPU:13, one launch (start us, length us, event | category | flops | bytes accessed | tf_op | source)
XLA Modules:
  0.0 82.7 jit_solution(5220681594467130341)
XLA Ops:
  0.0 0.0 copy-start
  0.0 1.2 %copy-done = f32[2,4,256,128]{3,2,1,0:T(8,128)S(1)} copy-done((f32[2,4,256,128]{3,2,1,0:T(8,128)S(1)}, f32[2,4,256,128]{3,2,1,0:T(8,128)}, u32[]{:S(2)}) %copy-start) | copy-done | bytes 1048600
  1.2 0.0 copy-start.1
  1.2 0.7 copy-done.1
  1.9 0.0 copy-start.2
  1.9 0.7 copy-done.2
  2.6 0.0 copy-start.3
  2.6 0.7 copy-done.3
  3.3 0.0 copy-start.4
  3.3 0.7 copy-done.4
  4.0 77.7 %shard_map.55 = f32[2,4,256,128]{3,2,1,0:T(8,128)S(1)} custom-call(f32[2,4,256,128]{3,2,1,0:T(8,128)S(1)} %copy-done, f32[2,4,128]{2,1,0:T(4,128)S(1)} %copy-done.1, s32[2,128]{1,0:T(2,128)S(1)} %copy-done.3, f32[2,4,128]{2,1,0:T(4,128)S(1)} %copy-done.2, f32[2,2]{1,0:T(2,128)S(1)} %copy-done.4), custom_call_target="tpu_custom_call" | custom-call | tf_op jit(solution)/shard_map/pallas_call | solution.py:462
  81.7 1.0 %copy.7 = f32[2,4,256,128]{3,2,1,0:T(8,128)} copy(f32[2,4,256,128]{3,2,1,0:T(8,128)S(1)} %shard_map.55) | data formatting | bytes 2097152
Async XLA Ops:
  0.0 1.2 %copy-start = (f32[2,4,256,128]{3,2,1,0:T(8,128)S(1)}, f32[2,4,256,128]{3,2,1,0:T(8,128)}, u32[]{:S(2)}) copy-start(f32[2,4,256,128]{3,2,1,0:T(8,128)} %state.1) | copy-start | bytes 3145732
  1.2 0.7 copy-start.1
  1.9 0.7 copy-start.2
  2.6 0.7 copy-start.3
  3.3 0.7 copy-start.4
where the time goes:
time: 82.9 us; the launch traced here: 82.7 us
  Pallas kernels  77.7 us (94%)
  local copies, waits for them, and re-layouts  4.93 us (6%)
    pallas_call x1, Pallas kernels, shards(): pl.pallas_call(functools.partial(kernel, (tm_n, half, L, R, K)), out_shap...  77.7 us
    unnamed x11, local copies, waits for them, and re-layouts  4.93 us

commit v1 on v0

--- a/solution.py
+++ b/solution.py
@@ -494,6 +494,434 @@
     )(state, far_field, face_index, face_weight, mean_flow)
 
 
+def skew_part(o, coef):
+    half = len(o)
+    quarter = half // 2
+
+    def at(n):
+        return o[n % half], -1.0 if (n // half) % 2 else 1.0
+
+    res = []
+    for n in range(half):
+        total = None
+        for m in range(1, quarter):
+            (a, sa), (b, sb) = at(n - m), at(n + m)
+            term = (coef[m] * sa) * (a - b if sa == sb else a + b)
+            total = term if total is None else total + term
+        a, sa = at(n - quarter)
+        term = (coef[quarter] * sa) * a
+        res.append(term if total is None else total + term)
+    return res
+
+
+def cyclic_part(e, coef):
+    half = len(e)
+    res = []
+    for n in range(half):
+        total = None
+        for m in range(1, half // 2):
+            term = coef[m] * (e[(n - m) % half] - e[(n + m) % half])
+            total = term if total is None else total + term
+        res.append(total)
+    return res
+
+
+def time_term_split(q, even, odd):
+    half = len(q) // 2
+    quarter = half // 2
+    e = [q[n] + q[n + half] for n in range(half)]
+    o = [q[n] - q[n + half] for n in range(half)]
+    ee = [e[n] + e[n + quarter] for n in range(quarter)]
+    eo = [e[n] - e[n + quarter] for n in range(quarter)]
+    low = [0.0] + [0.5 * (even[m] - even[quarter - m]) for m in range(1, quarter)]
+    high = [0.0] + [0.5 * (even[m] + even[quarter - m]) for m in range(1, quarter)]
+    cyc = cyclic_part(ee, low)
+    skw = skew_part(eo, high)
+    ev = [cyc[n] + skw[n] for n in range(quarter)] + [cyc[n] - skw[n] for n in range(quarter)]
+    od = skew_part(o, odd)
+    return [ev[n] + od[n] for n in range(half)] + [ev[n] - od[n] for n in range(half)]
+
+
+def ring_kernel(dims, state, far, fidx, fw, mf, out, q, tt, ff, wts, fi, lane_ix, blk_ix, ww, gg, fo, fg, mfs,
+                in_s, in_r, out_s, out_r, p_s, p_r, h_s, h_r, f_s, f_r, loc):
+    tm_n, half, L, R, K = dims
+    NT = tm_n * L
+    G = tm_n * half
+    cycle = half * 128
+    nsec = len(SECTION_FACTORS)
+    groups = 4 * NT // 8
+    me = lax.axis_index("tm")
+    blk = lax.axis_index("block")
+    side = lax.div(blk, half)
+    place = lax.rem(blk, half)
+    row0 = side * half
+
+    def slab(t, b):
+        return b * tm_n + jnp.where(lax.rem(b, 2) == 0, t, tm_n - 1 - t)
+
+    def owner(g):
+        b = lax.div(g, tm_n)
+        t = lax.rem(g, tm_n)
+        return jnp.where(lax.rem(b, 2) == 0, t, tm_n - 1 - t), b
+
+    g = slab(me, place)
+    seam = g == G - 1
+    prev_t, prev_b = owner(lax.rem(g + G - 1, G))
+    prev_dev = {"tm": prev_t, "block": row0 + prev_b}
+    seam_dev = {"tm": 0, "block": row0 + half - 1}
+    other_dev = {"block": (1 - side) * half + place}
+    here = me * half + place
+
+    def peer(t):
+        return lax.rem(here + 1 + t, G)
+
+    def dev(j):
+        return {"tm": lax.div(j, half), "block": row0 + lax.rem(j, half)}
+
+    def rows(j):
+        return pl.multiple_of(slab(lax.div(j, half), lax.rem(j, half)) * R, R)
+
+    def lev(t):
+        return pl.ds(t * L, L)
+
+    def rc(src, dst, ss, rs, to):
+        return pltpu.make_async_remote_copy(src_ref=src, dst_ref=dst, send_sem=ss, recv_sem=rs,
+                                            device_id=to, device_id_type=MESH)
+
+    bar = pltpu.get_barrier_semaphore()
+
+    @pl.loop(0, G - 1)
+    def _(t):
+        pl.semaphore_signal(bar, inc=1, device_id=dev(peer(t)), device_id_type=MESH)
+
+    @pl.when(seam)
+    def _():
+        pl.semaphore_signal(bar, inc=1, device_id=other_dev, device_id_type=MESH)
+
+    own = pltpu.make_async_copy(state.at[:, :, pl.ds(rows(here), R)], q.at[0, place, lev(me), :, pl.ds(0, R)], loc.at[0])
+    own.start()
+    own_mf = pltpu.make_async_copy(mf, mfs, loc.at[4])
+    own_mf.start()
+    pl.semaphore_wait(bar, G - 1 + jnp.where(seam, 1, 0))
+
+    def far_copy(j):
+        return rc(far, ff.at[lax.rem(j, half), lev(lax.div(j, half))], p_s.at[0], p_r.at[0, j], seam_dev)
+
+    def wt_copy(j):
+        return rc(fw, wts.at[lax.rem(j, half), lev(lax.div(j, half))], p_s.at[1], p_r.at[1, j], seam_dev)
+
+    def ix_copy(j):
+        return rc(fidx, fi.at[lax.rem(j, half), lax.div(j, half)], p_s.at[2], p_r.at[2, j], seam_dev)
+
+    own_far = pltpu.make_async_copy(far, ff.at[place, lev(me)], loc.at[1])
+    own_wt = pltpu.make_async_copy(fw, wts.at[place, lev(me)], loc.at[2])
+    own_ix = pltpu.make_async_copy(fidx, fi.at[place, me], loc.at[3])
+
+    @pl.when(seam)
+    def _():
+        own_far.start()
+        own_wt.start()
+        own_ix.start()
+
+    @pl.when(jnp.logical_not(seam))
+    def _():
+        far_copy(here).start()
+        wt_copy(here).start()
+        ix_copy(here).start()
+
+    def in_copy(j, src):
+        return rc(state.at[:, :, pl.ds(rows(j), R)],
+                  q.at[0, lax.rem(src, half), lev(lax.div(src, half)), :, pl.ds(0, R)],
+                  in_s.at[j], in_r.at[src], dev(j))
+
+    @pl.loop(0, G - 1)
+    def _(t):
+        in_copy(peer(t), here).start()
+
+    lane = lax.broadcasted_iota(jnp.int32, (8, 128), 1)
+    sub = lax.broadcasted_iota(jnp.int32, (8, 128), 0)
+    first_lane, last_lane = lane == 0, lane == 127
+
+    @pl.when(seam)
+    def _():
+        own_far.wait()
+        own_wt.wait()
+        own_ix.wait()
+
+        @pl.loop(0, G - 1)
+        def _(t):
+            j = peer(t)
+            far_copy(j).wait_recv()
+            wt_copy(j).wait_recv()
+            ix_copy(j).wait_recv()
+
+        for b in range(half):
+            @pl.loop(0, NT)
+            def _(l):
+                for v in range(4):
+                    gg[1, b, pl.ds(4 * l + v, 1)] = ff[b, l, pl.ds(v, 1)]
+
+            @pl.loop(0, NT // 2)
+            def _(m):
+                def ix(l):
+                    return jnp.broadcast_to(fi[b, lax.div(l, L), pl.ds(lax.rem(l, L), 1)], (8, 128))
+
+                def wt(l, k):
+                    return jnp.broadcast_to(wts[b, l, pl.ds(k, 1)], (8, 128))
+
+                start = jnp.where(sub < 4, ix(2 * m), ix(2 * m + 1))
+                at = pl.ds(8 * m, 8)
+                for k in range(K):
+                    src = start + k
+                    src = jnp.where(src >= cycle, src - cycle, src)
+                    lane_ix[k, b, at] = jnp.bitwise_and(src, 127)
+                    blk_ix[k, b, at] = lax.shift_right_logical(src, 7)
+                    ww[k, b, at] = jnp.where(sub < 4, wt(2 * m, k), wt(2 * m + 1, k))
+
+    own_mf.wait()
+    speed_u = jnp.where(side == 0, mfs[0, 0], mfs[1, 0])
+    speed_v = jnp.where(side == 0, mfs[0, 1], mfs[1, 1])
+
+    def trail(i):
+        s, lo, n = ([(0, 0, 2), (0, 2, 3)] + [(s, s, 2) for s in range(1, nsec)])[i]
+        return rc(q.at[s, :, :, :, pl.ds(lo, n)], q.at[s, :, :, :, pl.ds(R + lo, n)], h_s.at[i], h_r.at[i], prev_dev)
+
+    def face_copy(s):
+        return rc(fo.at[side, s], fg.at[s], f_s.at[s], f_r.at[s], other_dev)
+
+    def time_pass(s, w):
+        c = SECTION_FACTORS[s - 1]
+        even, odd = split_coefficients(NT, -OMEGA * c)
+        at = pl.ds(w, 8)
+
+        @pl.loop(0, 4)
+        def _(v):
+            for b in range(half):
+                xs = [q[s - 1, b, l, v, at] for l in range(NT)]
+                terms = time_term_split(xs, even, odd)
+                for l in range(NT):
+                    tt[b, l, v] = (q[0, b, l, v, at] + terms[l]) - (4.0 * DISSIPATION * c) * xs[l]
+
+    def space_pass(s, w, lo, hi, ghosts):
+        c = SECTION_FACTORS[s - 1]
+        hh = 0.5 * c
+        hu, hv = hh * speed_u, hh * speed_v
+        near = DISSIPATION * c
+        cu, cd, cr, cl = near - hu, near + hu, near - hv, near + hv
+        span = range(half)
+        if ghosts:
+            up_at = sub == jnp.where(seam, R - 1 - w, 8)
+            dn_at = sub == jnp.where(seam, R - w, 8)
+
+        def level(l):
+            di, dj, acc = [[], []], [[], []], [[], []]
+            di = [[None] * half for _ in range(4)]
+            dj = [[None] * half for _ in range(4)]
+            acc = [[None] * half for _ in range(4)]
+            for v in range(4):
+                x = [q[s - 1, b, l, v, pl.ds(w, 8)] for b in span]
+                rr = [pltpu.roll(x[b], 127, 1) for b in span]
+                rl = [pltpu.roll(x[b], 1, 1) for b in span]
+                for b in span:
+                    up = q[s - 1, b, l, v, pl.ds(w + 1, 8)]
+                    dn = q[s - 1, b, l, v, pl.ds(w - 1, 8)]
+                    if ghosts:
+                        at = pl.ds(4 * l + v, 1)
+                        up = jnp.where(up_at, jnp.broadcast_to(gg[side, b, at], (8, 128)), up)
+                        dn = jnp.where(dn_at, jnp.broadcast_to(gg[1 - side, b, at], (8, 128)), dn)
+                    right = jnp.where(last_lane, rr[(b + 1) % half], rr[b])
+                    left = jnp.where(first_lane, rl[(b - 1) % half], rl[b])
+                    acc[v][b] = (tt[b, l, v] + (cu * up + cd * dn)) + (cr * right + cl * left)
+                    if v in (1, 3):
+                        di[v][b] = up - dn
+                    if v in (2, 3):
+                        dj[v][b] = right - left
+            for b in span:
+                cross = hh * (di[1][b] + dj[2][b])
+                new = [acc[0][b] - cross, acc[1][b] - hh * di[3][b], acc[2][b] - hh * dj[3][b], acc[3][b] - cross]
+                for v in range(4):
+                    q[s, b, l, v, pl.ds(w + lo, hi - lo)] = new[v][lo:hi]
+                    if ghosts and s < nsec:
+                        for k in range(2):
+                            row = R - 1 + k - w
+                            fo[k, s, b, pl.ds(4 * l + v, 1)] = new[v][row:row + 1]
+
+        @pl.loop(0, NT // 2)
+        def _(i):
+            for j in range(2):
+                level(2 * i + j)
+
+    own.wait()
+
+    @pl.loop(0, G - 1)
+    def _(t):
+        j = peer(G - 2 - t)
+        in_copy(j, j).wait_recv()
+
+    trail(0).start()
+    trail(1).start()
+
+    def rise(s):
+        if 2 * s + 8 < R:
+            windows = [(s, 0, 8), (R - 8 - s, 0, 8)]
+        else:
+            w = (R - 8) // 2
+            windows = [(w, s - w, R - s - w)]
+        for w, lo, hi in windows:
+            time_pass(s, w)
+            space_pass(s, w, lo, hi, False)
+
+    def fall(s):
+        if s < nsec:
+            windows = [(R - 8 + s, 8 - 2 * s, 8)]
+        else:
+            windows = [(R - s, 0, 8), (R + s - 8, 16 - 2 * s, 8)]
+        for w, lo, hi in windows:
+            time_pass(s, w)
+            space_pass(s, w, lo, hi, True)
+
+    def out_copy(i, j, src):
+        lo, n = [(nsec, R - 2 * nsec), (R - nsec, nsec), (R, nsec)][i]
+        g_src = slab(lax.div(src, half), lax.rem(src, half))
+        to = g_src * R + lo if i < 2 else lax.rem(g_src + 1, G) * R
+        return rc(q.at[nsec, lax.rem(j, half), lev(lax.div(j, half)), :, pl.ds(lo, n)],
+                  out.at[:, :, pl.ds(to, n)], out_s.at[i, j], out_r.at[i, src], dev(j))
+
+    def own_out(i):
+        lo, n = [(nsec, R - 2 * nsec), (R - nsec, nsec), (R, nsec)][i]
+        to = g * R + lo if i < 2 else lax.rem(g + 1, G) * R
+        return pltpu.make_async_copy(q.at[nsec, place, lev(me), :, pl.ds(lo, n)], out.at[:, :, pl.ds(to, n)], loc.at[5 + i])
+
+    def send_out(i):
+        @pl.loop(0, G - 1)
+        def _(t):
+            out_copy(i, peer(t), here).start()
+
+        own_out(i).start()
+
+    for s in range(1, nsec + 1):
+        rise(s)
+        if s < nsec:
+            trail(s + 1).start()
+        if s == 3:
+            trail(0).wait_recv()
+
+            @pl.when(seam)
+            def _():
+                @pl.loop(0, NT)
+                def _(l):
+                    for b in range(half):
+                        for v in range(4):
+                            for k in range(2):
+                                fo[k, 0, b, pl.ds(4 * l + v, 1)] = q[0, b, l, v, pl.ds(R - 1 + k, 1)]
+
+                face_copy(0).start()
+    send_out(0)
+
+    for s in range(1, nsec + 1):
+        if s > 1:
+            trail(s).wait_recv()
+        if s == 2:
+            trail(1).wait_recv()
+
+        @pl.when(seam)
+        def _():
+            face_copy(s - 1).wait_recv()
+
+            @pl.loop(0, groups)
+            def _(m):
+                at = pl.ds(8 * m, 8)
+                for b in range(half):
+                    total = jnp.zeros((8, 128), jnp.float32)
+                    for k in range(K):
+                        picked = jnp.zeros((8, 128), jnp.float32)
+                        for h in range(half):
+                            got = jnp.take_along_axis(fg[s - 1, h, at], lane_ix[k, b, at], axis=1)
+                            picked = jnp.where(blk_ix[k, b, at] == h, got, picked)
+                        total = total + ww[k, b, at] * picked
+                    gg[0, b, at] = total
+
+        fall(s)
+        if s < nsec:
+            @pl.when(seam)
+            def _():
+                face_copy(s).start()
+    send_out(1)
+    send_out(2)
+
+    for i in range(3):
+        @pl.loop(0, G - 1)
+        def _(t):
+            j = peer(t)
+            out_copy(i, j, j).wait_recv()
+
+        own_out(i).wait()
+
+    @pl.loop(0, G - 1)
+    def _(t):
+        j = peer(t)
+        in_copy(j, here).wait_send()
+        for i in range(3):
+            out_copy(i, j, here).wait_send()
+
+    for i in range(nsec + 1):
+        trail(i).wait_send()
+
+    @pl.when(jnp.logical_not(seam))
+    def _():
+        far_copy(here).wait_send()
+        wt_copy(here).wait_send()
+        ix_copy(here).wait_send()
+
+    @pl.when(seam)
+    def _():
+        for s in range(nsec):
+            face_copy(s).wait_send()
+
+
+def ring_shards(dims, state, far_field, face_index, face_weight, mean_flow):
+    tm_n, half = dims
+    L, _, rows, width = state.shape
+    K = face_weight.shape[1]
+    G = tm_n * half
+    R = rows // G
+    NT = L * tm_n
+    n = len(SECTION_FACTORS)
+    f32 = jnp.float32
+    hbm = pl.BlockSpec(memory_space=pl.ANY)
+    dma = pltpu.SemaphoreType.DMA
+    V = pltpu.VMEM
+    args = [pltpu.with_memory_space_constraint(a, pltpu.HBM)
+            for a in (state, far_field, face_index, face_weight, mean_flow)]
+    return pl.pallas_call(
+        functools.partial(ring_kernel, (tm_n, half, L, R, K)),
+        out_shape=jax.ShapeDtypeStruct(state.shape, f32),
+        in_specs=[hbm] * 5,
+        out_specs=hbm,
+        scratch_shapes=[
+            V((n + 1, half, NT, 4, R + 8, width), f32),
+            V((half, NT, 4, 8, width), f32),
+            V((half, NT, 4, width), f32),
+            V((half, NT, K, width), f32),
+            V((half, tm_n, L, width), jnp.int32),
+            V((K, half, 4 * NT, width), jnp.int32),
+            V((K, half, 4 * NT, width), jnp.int32),
+            V((K, half, 4 * NT, width), f32),
+            V((2, half, 4 * NT, width), f32),
+            V((2, n, half, 4 * NT, width), f32),
+            V((n, half, 4 * NT, width), f32),
+            pltpu.SMEM((2, 2), f32),
+            dma((G,)), dma((G,)), dma((3, G)), dma((3, G)),
+            dma((3,)), dma((3, G)),
+            dma((n + 1,)), dma((n + 1,)),
+            dma((n,)), dma((n,)),
+            dma((8,)),
+        ],
+        compiler_params=pltpu.CompilerParams(
+            collective_id=0, has_side_effects=True, vmem_limit_bytes=48 * 1024 * 1024),
+    )(*args)
+
+
 def solution(mesh):
     dims = (mesh.shape["tm"], mesh.shape["block"] // 2)
     in_specs = (
@@ -504,5 +932,11 @@
         P(),
     )
     out_specs = P("tm", None, None, "block")
-    return jax.shard_map(functools.partial(shards, dims), mesh=mesh, in_specs=in_specs,
-                         out_specs=out_specs, check_vma=False)
+
+    def body(state, *rest):
+        ring = dims[0] * dims[1]
+        levels = state.shape[0] * dims[0]
+        fits = state.shape[2] == 16 * ring and state.shape[3] == 128 and dims[1] % 2 == 0 and levels % 8 == 0
+        return (ring_shards if fits else shards)(dims, state, *rest)
+
+    return jax.shard_map(body, mesh=mesh, in_specs=in_specs, out_specs=out_specs, check_vma=False)

time: 82.9 us -> 66.7 us (0.80)
  the two profiles are of different devices: /device:TPU:13 before, /device:TPU:25 now
where the time goes in v1:
time: 66.7 us; the launch traced here: 66.5 us
  Pallas kernels  65.5 us (98%)
  local copies, waits for them, and re-layouts  0.97 us (1%)
    pallas_call x1, Pallas kernels, ring_shards(): pl.pallas_call(functools.partial(ring_kernel, (tm_n, half, L, R, K)), out...  65.5 us

profile of v1, /device:TPU:25, one launch (start us, length us, event | category | flops | bytes accessed | tf_op | source)
XLA Modules:
  0.0 66.5 jit_solution(2616873075592029771)
XLA Ops:
  0.0 65.5 %shard_map.55 = f32[2,4,256,128]{3,2,1,0:T(8,128)S(1)} custom-call(f32[2,4,256,128]{3,2,1,0:T(8,128)} %state.1, f32[2,4,128]{2,1,0:T(4,128)} %far.1, s32[2,128]{1,0:T(2,128)} %fidx.1, f32[2,4,128]{2,1,0:T(4,128)} %fw.1, f32[2,2]{1,0:T(2,128)} %mf.1), custom_call_target="tpu_custom_call" | custom-call | tf_op jit(solution)/shard_map/pallas_call | solution.py:896
  65.5 1.0 %copy.7 = f32[2,4,256,128]{3,2,1,0:T(8,128)} copy(f32[2,4,256,128]{3,2,1,0:T(8,128)S(1)} %shard_map.55) | data formatting | bytes 2097152

commit v2 on v0

--- a/solution.py
+++ b/solution.py
@@ -494,6 +494,560 @@
     )(state, far_field, face_index, face_weight, mean_flow)
 
 
+def skew_part(o, coef):
+    half = len(o)
+    quarter = half // 2
+
+    def at(n):
+        return o[n % half], -1.0 if (n // half) % 2 else 1.0
+
+    res = []
+    for n in range(half):
+        total = None
+        for m in range(1, quarter):
+            (a, sa), (b, sb) = at(n - m), at(n + m)
+            term = (coef[m] * sa) * (a - b if sa == sb else a + b)
+            total = term if total is None else total + term
+        a, sa = at(n - quarter)
+        term = (coef[quarter] * sa) * a
+        res.append(term if total is None else total + term)
+    return res
+
+
+def cyclic_part(e, coef):
+    half = len(e)
+    res = []
+    for n in range(half):
+        total = None
+        for m in range(1, half // 2):
+            term = coef[m] * (e[(n - m) % half] - e[(n + m) % half])
+            total = term if total is None else total + term
+        res.append(total)
+    return res
+
+
+def time_term_split(q, even, odd):
+    half = len(q) // 2
+    quarter = half // 2
+    e = [q[n] + q[n + half] for n in range(half)]
+    o = [q[n] - q[n + half] for n in range(half)]
+    ee = [e[n] + e[n + quarter] for n in range(quarter)]
+    eo = [e[n] - e[n + quarter] for n in range(quarter)]
+    low = [0.0] + [0.5 * (even[m] - even[quarter - m]) for m in range(1, quarter)]
+    high = [0.0] + [0.5 * (even[m] + even[quarter - m]) for m in range(1, quarter)]
+    cyc = cyclic_part(ee, low)
+    skw = skew_part(eo, high)
+    ev = [cyc[n] + skw[n] for n in range(quarter)] + [cyc[n] - skw[n] for n in range(quarter)]
+    od = skew_part(o, odd)
+    return [ev[n] + od[n] for n in range(half)] + [ev[n] - od[n] for n in range(half)]
+
+
+def ring_kernel(dims, state, far, fidx, fw, mf, out, q, tt, ff, wts, fi, lane_ix, blk_ix, ww, gg, fo, mfs,
+                in_s, in_r, dup_s, dup_r, out_s, out_r, p_s, p_r, h_s, h_r, loc):
+    tm_n, half, L, R, K = dims
+    NT = tm_n * L
+    G = tm_n * half
+    Z = tm_n // 2
+    cycle = half * 128
+    nsec = len(SECTION_FACTORS)
+    reach = 2 * nsec
+    groups = 4 * NT // 8
+    me = lax.axis_index("tm")
+    blk = lax.axis_index("block")
+    side = lax.div(blk, half)
+    place = lax.rem(blk, half)
+
+    def slab(t, b, sd):
+        z = lax.div(t, 2)
+        c = lax.rem(t, 2)
+        zo = jnp.where(sd == 0, z, Z - 1 - z)
+        return 4 * zo + jnp.where(lax.rem(b + zo, 2) == 0, c, 3 - c)
+
+    def owner(g, sd):
+        zo = g // 4 if isinstance(g, int) else lax.div(g, 4)
+        k = g % 4 if isinstance(g, int) else lax.rem(g, 4)
+        xo = jnp.where(k >= 2, 1, 0)
+        c = jnp.where(k >= 2, 3 - k, k)
+        b = lax.rem(xo + zo, 2)
+        return 2 * jnp.where(sd == 0, zo, Z - 1 - zo) + c, b
+
+    def device(g, sd):
+        t, b = owner(g, sd)
+        return {"tm": t, "block": sd * half + b}
+
+    g = slab(me, place, side)
+    here = me * half + place
+    seam = g == G - 1
+    mixes = seam & (side == 0)
+    ends = seam & (side == 1)
+    mix_dev = device(G - 1, 0)
+    end_dev = device(G - 1, 1)
+    dup_list = [4 * z + 3 for z in range(1, Z - 1)]
+
+    def is_dup(x):
+        hit = x < -1
+        for d in dup_list:
+            hit = hit | (x == d)
+        return hit
+
+    takes_dup = is_dup(g)
+    feeds_prev = jnp.logical_not(is_dup(g - 1))
+    prev_side = jnp.where(g == 0, 1 - side, side)
+    prev_dev = device(lax.rem(g + G - 1, G), prev_side)
+    next_side = jnp.where(seam, 1 - side, side)
+
+    def peer(t):
+        return lax.rem(here + 1 + t, G)
+
+    def dev(j, sd):
+        return {"tm": lax.div(j, half), "block": sd * half + lax.rem(j, half)}
+
+    def slab_of(j):
+        return slab(lax.div(j, half), lax.rem(j, half), side)
+
+    def lev(t):
+        return pl.ds(t * L, L)
+
+    def rc(src, dst, ss, rs, to):
+        return pltpu.make_async_remote_copy(src_ref=src, dst_ref=dst, send_sem=ss, recv_sem=rs,
+                                            device_id=to, device_id_type=MESH)
+
+    bar = pltpu.get_barrier_semaphore()
+
+    @pl.loop(0, G - 1)
+    def _(t):
+        pl.semaphore_signal(bar, inc=1, device_id=dev(peer(t), side), device_id_type=MESH)
+
+    @pl.when(seam)
+    def _():
+        @pl.loop(0, G)
+        def _(j):
+            pl.semaphore_signal(bar, inc=1, device_id=dev(j, 1 - side), device_id_type=MESH)
+
+    @pl.when(jnp.logical_not(seam))
+    def _():
+        pl.semaphore_signal(bar, inc=1, device_id=device(G - 1, 1 - side), device_id_type=MESH)
+
+    own = pltpu.make_async_copy(state.at[:, :, pl.ds(pl.multiple_of(g * R, R), R)],
+                                q.at[0, place, lev(me), :, pl.ds(0, R)], loc.at[0])
+    own.start()
+    own_mf = pltpu.make_async_copy(mf, mfs, loc.at[4])
+    own_mf.start()
+
+    def ahead_rows(d):
+        return state.at[:, :, pl.ds((d + 1) * R, reach)]
+
+    def ahead_spot(j):
+        return q.at[0, lax.rem(j, half), lev(lax.div(j, half)), :, pl.ds(R, reach)]
+
+    def dup_copy(i, j):
+        return rc(ahead_rows(dup_list[i]), ahead_spot(j), dup_s.at[i], dup_r.at[j], device(dup_list[i], side))
+
+    def own_dup(i):
+        return pltpu.make_async_copy(ahead_rows(dup_list[i]), ahead_spot(here), loc.at[5])
+
+    for i, d in enumerate(dup_list):
+        @pl.when(g == d)
+        def _():
+            own_dup(i).start()
+
+    pl.semaphore_wait(bar, G + jnp.where(seam, G - 1, 0))
+
+    def far_copy(j, sd):
+        return rc(far, ff.at[sd, lax.rem(j, half), lev(lax.div(j, half))], p_s.at[0], p_r.at[0, sd * G + j], end_dev)
+
+    def wt_copy(j, sd):
+        return rc(fw, wts.at[sd, lax.rem(j, half), lev(lax.div(j, half))], p_s.at[1], p_r.at[1, sd * G + j], mix_dev)
+
+    def ix_copy(j, sd):
+        return rc(fidx, fi.at[sd, lax.rem(j, half), lax.div(j, half)], p_s.at[2], p_r.at[2, sd * G + j], mix_dev)
+
+    own_far = pltpu.make_async_copy(far, ff.at[side, place, lev(me)], loc.at[1])
+    own_wt = pltpu.make_async_copy(fw, wts.at[side, place, lev(me)], loc.at[2])
+    own_ix = pltpu.make_async_copy(fidx, fi.at[side, place, me], loc.at[3])
+
+    @pl.when(ends)
+    def _():
+        own_far.start()
+
+    @pl.when(jnp.logical_not(ends))
+    def _():
+        far_copy(here, side).start()
+
+    @pl.when(mixes)
+    def _():
+        own_wt.start()
+        own_ix.start()
+
+    @pl.when(jnp.logical_not(mixes))
+    def _():
+        wt_copy(here, side).start()
+        ix_copy(here, side).start()
+
+    parts = ((0, reach), (reach, R - reach))
+
+    def in_copy(i, j, src):
+        lo, n = parts[i]
+        return rc(state.at[:, :, pl.ds(slab_of(j) * R + lo, n)],
+                  q.at[0, lax.rem(src, half), lev(lax.div(src, half)), :, pl.ds(lo, n)],
+                  in_s.at[i, j], in_r.at[i, src], dev(j, side))
+
+    @pl.loop(0, G - 1)
+    def _(t):
+        in_copy(0, peer(t), here).start()
+
+    for i, d in enumerate(dup_list):
+        @pl.when(g != d)
+        def _():
+            dup_copy(i, here).start()
+
+    @pl.loop(0, G - 1)
+    def _(t):
+        in_copy(1, peer(t), here).start()
+
+    lane = lax.broadcasted_iota(jnp.int32, (8, 128), 1)
+    sub = lax.broadcasted_iota(jnp.int32, (8, 128), 0)
+    first_lane, last_lane = lane == 0, lane == 127
+
+    def others(sd):
+        def each(body):
+            @pl.loop(0, G - 1)
+            def _(t):
+                body(peer(t), sd)
+
+            @pl.loop(0, G)
+            def _(j):
+                body(j, 1 - sd)
+        return each
+
+    @pl.when(ends)
+    def _():
+        own_far.wait()
+
+        @others(1)
+        def _(j, sd):
+            far_copy(j, sd).wait_recv()
+
+        for k in range(2):
+            for b in range(half):
+                @pl.loop(0, NT)
+                def _(l):
+                    for v in range(4):
+                        gg[k, b, pl.ds(4 * l + v, 1)] = ff[1 - k, b, l, pl.ds(v, 1)]
+
+    @pl.when(mixes)
+    def _():
+        own_wt.wait()
+        own_ix.wait()
+
+        @others(0)
+        def _(j, sd):
+            wt_copy(j, sd).wait_recv()
+            ix_copy(j, sd).wait_recv()
+
+        for r in range(2):
+            for b in range(half):
+                @pl.loop(0, NT // 2)
+                def _(m):
+                    def ix(l):
+                        return jnp.broadcast_to(fi[r, b, lax.div(l, L), pl.ds(lax.rem(l, L), 1)], (8, 128))
+
+                    def wt(l, k):
+                        return jnp.broadcast_to(wts[r, b, l, pl.ds(k, 1)], (8, 128))
+
+                    start = jnp.where(sub < 4, ix(2 * m), ix(2 * m + 1))
+                    at = pl.ds(8 * m, 8)
+                    for k in range(K):
+                        src = start + k
+                        src = jnp.where(src >= cycle, src - cycle, src)
+                        lane_ix[r, k, b, at] = jnp.bitwise_and(src, 127)
+                        blk_ix[r, k, b, at] = lax.shift_right_logical(src, 7)
+                        ww[r, k, b, at] = jnp.where(sub < 4, wt(2 * m, k), wt(2 * m + 1, k))
+
+    own_mf.wait()
+
+    def speeds(sd):
+        return jnp.where(sd == 0, mfs[0, 0], mfs[1, 0]), jnp.where(sd == 0, mfs[0, 1], mfs[1, 1])
+
+    own_speed = speeds(side)
+    next_speed = speeds(next_side)
+
+    def feed():
+        return rc(q.at[0, :, :, :, pl.ds(0, reach)], q.at[0, :, :, :, pl.ds(R, reach)], h_s.at[0], h_r.at[0], prev_dev)
+
+    def time_pass(s, w):
+        c = SECTION_FACTORS[s - 1]
+        even, odd = split_coefficients(NT, -OMEGA * c)
+        at = pl.ds(w, 8)
+
+        @pl.loop(0, 4)
+        def _(v):
+            for b in range(half):
+                xs = [q[s - 1, b, l, v, at] for l in range(NT)]
+                terms = time_term_split(xs, even, odd)
+                for l in range(NT):
+                    tt[b, l, v] = (q[0, b, l, v, at] + terms[l]) - (4.0 * DISSIPATION * c) * xs[l]
+
+    def space_pass(s, w, lo, hi, ghosts=False, border=False):
+        c = SECTION_FACTORS[s - 1]
+        hh = 0.5 * c
+        near = DISSIPATION * c
+
+        def weights(uv):
+            return near - hh * uv[0], near + hh * uv[0], near - hh * uv[1], near + hh * uv[1]
+
+        cu, cd, cr, cl = weights(own_speed)
+        if border:
+            beyond = sub >= R - w
+            cu, cd, cr, cl = [jnp.where(beyond, n, o) for n, o in zip(weights(next_speed), (cu, cd, cr, cl))]
+        span = range(half)
+        if ghosts:
+            up_at = sub == jnp.where(seam, R - 1 - w, 8)
+            dn_at = sub == jnp.where(seam, R - w, 8)
+
+        def level(l):
+            di = [[None] * half for _ in range(4)]
+            dj = [[None] * half for _ in range(4)]
+            acc = [[None] * half for _ in range(4)]
+            for v in range(4):
+                x = [q[s - 1, b, l, v, pl.ds(w, 8)] for b in span]
+                rr = [pltpu.roll(x[b], 127, 1) for b in span]
+                rl = [pltpu.roll(x[b], 1, 1) for b in span]
+                for b in span:
+                    up = q[s - 1, b, l, v, pl.ds(w + 1, 8)]
+                    dn = q[s - 1, b, l, v, pl.ds(w - 1, 8)]
+                    if ghosts:
+                        at = pl.ds(4 * l + v, 1)
+                        up = jnp.where(up_at, jnp.broadcast_to(gg[0, b, at], (8, 128)), up)
+                        dn = jnp.where(dn_at, jnp.broadcast_to(gg[1, b, at], (8, 128)), dn)
+                    right = jnp.where(last_lane, rr[(b + 1) % half], rr[b])
+                    left = jnp.where(first_lane, rl[(b - 1) % half], rl[b])
+                    acc[v][b] = (tt[b, l, v] + (cu * up + cd * dn)) + (cr * right + cl * left)
+                    if v in (1, 3):
+                        di[v][b] = up - dn
+                    if v in (2, 3):
+                        dj[v][b] = right - left
+            for b in span:
+                cross = hh * (di[1][b] + dj[2][b])
+                new = [acc[0][b] - cross, acc[1][b] - hh * di[3][b], acc[2][b] - hh * dj[3][b], acc[3][b] - cross]
+                for v in range(4):
+                    q[s, b, l, v, pl.ds(w + lo, hi - lo)] = new[v][lo:hi]
+                    if ghosts and s < nsec:
+                        for k in range(2):
+                            row = R - 1 + k - w
+                            fo[k, b, pl.ds(4 * l + v, 1)] = new[v][row:row + 1]
+
+        @pl.loop(0, NT // 4)
+        def _(i):
+            for j in range(4):
+                level(4 * i + j)
+
+    own.wait()
+
+    @pl.loop(0, G - 1)
+    def _(t):
+        j = peer(G - 2 - t)
+        in_copy(0, j, j).wait_recv()
+
+    @pl.when(feeds_prev)
+    def _():
+        feed().start()
+
+    for s in range(1, 4):
+        w = min(s, reach - 8)
+        time_pass(s, w)
+        space_pass(s, w, s - w, reach - s - w)
+
+    @pl.loop(0, G - 1)
+    def _(t):
+        j = peer(G - 2 - t)
+        in_copy(1, j, j).wait_recv()
+
+    for s in range(1, nsec + 1):
+        if s < 4:
+            w = R - 8 - s
+            lo, hi = reach - s - w, 8
+        else:
+            w = (R - 8) // 2
+            lo, hi = s - w, R - s - w
+        time_pass(s, w)
+        space_pass(s, w, lo, hi)
+
+    spans = ((nsec, R - 2 * nsec), (R - nsec, nsec), (R, nsec))
+
+    def result(i, j):
+        lo, n = spans[i]
+        return q.at[nsec, lax.rem(j, half), lev(lax.div(j, half)), :, pl.ds(lo, n)]
+
+    def spot(i, gs):
+        lo, n = spans[i]
+        return out.at[:, :, pl.ds(gs * R + (lo if i < 2 else 0), n)]
+
+    def out_copy(i, j, gs):
+        return rc(result(i, j), spot(i, gs), out_s.at[i, j], out_r.at[i, gs], dev(j, side if i < 2 else next_side))
+
+    def own_out(i, gs):
+        return pltpu.make_async_copy(result(i, here), spot(i, gs), loc.at[5 + i])
+
+    following = lax.rem(g + 1, G)
+    takes_own = jnp.logical_not(seam)
+
+    @pl.loop(0, G - 1)
+    def _(t):
+        out_copy(0, peer(t), g).start()
+
+    for i, d in enumerate(dup_list):
+        @pl.when(g == d)
+        def _():
+            own_dup(i).wait()
+
+    @pl.when(takes_dup)
+    def _():
+        @pl.loop(0, G - 1)
+        def _(t):
+            dup_copy(0, peer(t)).wait_recv()
+
+    @pl.when(jnp.logical_not(takes_dup))
+    def _():
+        feed().wait_recv()
+
+    own_out(0, g).start()
+
+    @pl.when(mixes)
+    def _():
+        @pl.loop(0, NT)
+        def _(l):
+            for b in range(half):
+                for v in range(4):
+                    for k in range(2):
+                        fo[k, b, pl.ds(4 * l + v, 1)] = q[0, b, l, v, pl.ds(R - 1 + k, 1)]
+
+    for s in range(1, nsec + 1):
+        @pl.when(mixes)
+        def _():
+            @pl.loop(0, groups)
+            def _(m):
+                at = pl.ds(pl.multiple_of(8 * m, 8), 8)
+                for r in range(2):
+                    for b in range(half):
+                        total = jnp.zeros((8, 128), jnp.float32)
+                        for k in range(K):
+                            picked = jnp.zeros((8, 128), jnp.float32)
+                            for h in range(half):
+                                got = jnp.take_along_axis(fo[1 - r, h, at], lane_ix[r, k, b, at], axis=1)
+                                picked = jnp.where(blk_ix[r, k, b, at] == h, got, picked)
+                            total = total + ww[r, k, b, at] * picked
+                        gg[r, b, at] = total
+
+        time_pass(s, R - s)
+        space_pass(s, R - s, 0, 8, True, True)
+        time_pass(s, R + 2 - s)
+        space_pass(s, R + 2 - s, 6, 8, False, True)
+
+    @pl.loop(0, G - 1)
+    def _(t):
+        out_copy(1, peer(t), g).start()
+        out_copy(2, peer(t), following).start()
+
+    own_out(1, g).start()
+
+    @pl.when(takes_own)
+    def _():
+        own_out(2, following).start()
+
+    @pl.when(seam)
+    def _():
+        out_copy(2, here, following).start()
+
+    @pl.loop(0, G - 1)
+    def _(t):
+        gs = lax.rem(g + 1 + t, G)
+        out_copy(0, here, gs).wait_recv()
+        out_copy(1, here, gs).wait_recv()
+        out_copy(2, here, lax.rem(gs + 1, G)).wait_recv()
+
+    @pl.when(takes_own)
+    def _():
+        own_out(2, following).wait()
+
+    @pl.when(seam)
+    def _():
+        out_copy(2, here, following).wait_recv()
+        out_copy(2, here, following).wait_send()
+
+    own_out(0, g).wait()
+    own_out(1, g).wait()
+
+    @pl.loop(0, G - 1)
+    def _(t):
+        j = peer(t)
+        in_copy(0, j, here).wait_send()
+        in_copy(1, j, here).wait_send()
+        for i in range(3):
+            out_copy(i, j, g).wait_send()
+
+    for i, d in enumerate(dup_list):
+        @pl.when(g != d)
+        def _():
+            dup_copy(i, here).wait_send()
+
+    @pl.when(feeds_prev)
+    def _():
+        feed().wait_send()
+
+    @pl.when(jnp.logical_not(ends))
+    def _():
+        far_copy(here, side).wait_send()
+
+    @pl.when(jnp.logical_not(mixes))
+    def _():
+        wt_copy(here, side).wait_send()
+        ix_copy(here, side).wait_send()
+
+
+def ring_shards(dims, state, far_field, face_index, face_weight, mean_flow):
+    tm_n, half = dims
+    L, _, rows, width = state.shape
+    K = face_weight.shape[1]
+    G = tm_n * half
+    R = rows // G
+    NT = L * tm_n
+    n = len(SECTION_FACTORS)
+    f32 = jnp.float32
+    hbm = pl.BlockSpec(memory_space=pl.ANY)
+    dma = pltpu.SemaphoreType.DMA
+    V = pltpu.VMEM
+    args = [pltpu.with_memory_space_constraint(a, pltpu.HBM)
+            for a in (state, far_field, face_index, face_weight, mean_flow)]
+    return pl.pallas_call(
+        functools.partial(ring_kernel, (tm_n, half, L, R, K)),
+        out_shape=jax.ShapeDtypeStruct(state.shape, f32),
+        in_specs=[hbm] * 5,
+        out_specs=hbm,
+        scratch_shapes=[
+            V((n + 1, half, NT, 4, R + 16, width), f32),
+            V((half, NT, 4, 8, width), f32),
+            V((2, half, NT, 4, width), f32),
+            V((2, half, NT, K, width), f32),
+            V((2, half, tm_n, L, width), jnp.int32),
+            V((2, K, half, 4 * NT, width), jnp.int32),
+            V((2, K, half, 4 * NT, width), jnp.int32),
+            V((2, K, half, 4 * NT, width), f32),
+            V((2, half, 4 * NT, width), f32),
+            V((2, half, 4 * NT, width), f32),
+            pltpu.SMEM((2, 2), f32),
+            dma((2, G)), dma((2, G)),
+            dma((tm_n,)), dma((G,)),
+            dma((3, G)), dma((3, G)),
+            dma((3,)), dma((3, 2 * G)),
+            dma((1,)), dma((1,)),
+            dma((8,)),
+        ],
+        compiler_params=pltpu.CompilerParams(
+            collective_id=0, has_side_effects=True, vmem_limit_bytes=48 * 1024 * 1024),
+    )(*args)
+
+
 def solution(mesh):
     dims = (mesh.shape["tm"], mesh.shape["block"] // 2)
     in_specs = (
@@ -504,5 +1058,11 @@
         P(),
     )
     out_specs = P("tm", None, None, "block")
-    return jax.shard_map(functools.partial(shards, dims), mesh=mesh, in_specs=in_specs,
-                         out_specs=out_specs, check_vma=False)
+
+    def body(state, *rest):
+        tm_n, half = dims
+        fits = (half == 2 and tm_n % 2 == 0 and tm_n >= 4 and state.shape[2] == 16 * tm_n * half
+                and state.shape[3] == 128 and state.shape[0] * tm_n % 8 == 0)
+        return (ring_shards if fits else shards)(dims, state, *rest)
+
+    return jax.shard_map(body, mesh=mesh, in_specs=in_specs, out_specs=out_specs, check_vma=False)

time: 82.9 us -> 61.6 us (0.74)
  the two profiles are of different devices: /device:TPU:13 before, /device:TPU:25 now
where the time goes in v2:
time: 61.6 us; the launch traced here: 61.4 us
  Pallas kernels  60.5 us (98%)
  local copies, waits for them, and re-layouts  0.97 us (2%)
    pallas_call x1, Pallas kernels, ring_shards(): pl.pallas_call(functools.partial(ring_kernel, (tm_n, half, L, R, K)), out...  60.5 us

profile of v2, /device:TPU:25, one launch (start us, length us, event | category | flops | bytes accessed | tf_op | source)
XLA Modules:
  0.0 61.4 jit_solution(16756009545490820610)
XLA Ops:
  0.0 60.5 %shard_map.55 = f32[2,4,256,128]{3,2,1,0:T(8,128)S(1)} custom-call(f32[2,4,256,128]{3,2,1,0:T(8,128)} %state.1, f32[2,4,128]{2,1,0:T(4,128)} %far.1, s32[2,128]{1,0:T(2,128)} %fidx.1, f32[2,4,128]{2,1,0:T(4,128)} %fw.1, f32[2,2]{1,0:T(2,128)} %mf.1), custom_call_target="tpu_custom_call" | custom-call | tf_op jit(solution)/shard_map/pallas_call | solution.py:1022
  60.5 1.0 %copy.7 = f32[2,4,256,128]{3,2,1,0:T(8,128)} copy(f32[2,4,256,128]{3,2,1,0:T(8,128)S(1)} %shard_map.55) | data formatting | bytes 2097152

commit v3 on v2

--- a/solution.py
+++ b/solution.py
@@ -12,6 +12,7 @@
 OMEGA = 1.0
 DISSIPATION = 0.2
 PAD = 8
+FIRST_ROWS = 11
 MESH = pl.DeviceIdType.MESH
 
 
@@ -612,6 +613,15 @@
         return pltpu.make_async_remote_copy(src_ref=src, dst_ref=dst, send_sem=ss, recv_sem=rs,
                                             device_id=to, device_id_type=MESH)
 
+    def gather_of(n, whole=False):
+        return q.at[0, :, pl.ds(0, NT if whole else NT - L // half), :, pl.ds(0, n)]
+
+    def received(view, sem):
+        rc(view, view, p_s.at[0], sem, end_dev).wait_recv()
+
+    def sent(view, sem):
+        rc(view, view, sem, p_r.at[0], end_dev).wait_send()
+
     bar = pltpu.get_barrier_semaphore()
 
     @pl.loop(0, G - 1)
@@ -634,17 +644,30 @@
     own_mf = pltpu.make_async_copy(mf, mfs, loc.at[4])
     own_mf.start()
 
-    def ahead_rows(d):
-        return state.at[:, :, pl.ds((d + 1) * R, reach)]
-
-    def ahead_spot(j):
-        return q.at[0, lax.rem(j, half), lev(lax.div(j, half)), :, pl.ds(R, reach)]
-
-    def dup_copy(i, j):
-        return rc(ahead_rows(dup_list[i]), ahead_spot(j), dup_s.at[i], dup_r.at[j], device(dup_list[i], side))
+    first = FIRST_ROWS
+    parts = ((0, first), (first, R - first))
+    ahead = ((0, first - 8), (first - 8, reach + 8 - first), (0, reach))
+
+    def ahead_rows(d, k):
+        lo, n = ahead[k]
+        return state.at[:, :, pl.ds((d + 1) * R + lo, n)]
+
+    def ahead_spot(j, k):
+        lo, n = ahead[k]
+        return q.at[0, lax.rem(j, half), lev(lax.div(j, half)), :, pl.ds(R + lo, n)]
+
+    def dup_copy(i, k, j):
+        return rc(ahead_rows(dup_list[i], k), ahead_spot(j, k), dup_s.at[i, k], dup_r.at[k],
+                  device(dup_list[i], side))
 
     def own_dup(i):
-        return pltpu.make_async_copy(ahead_rows(dup_list[i]), ahead_spot(here), loc.at[5])
+        return pltpu.make_async_copy(ahead_rows(dup_list[i], 2), ahead_spot(here, 2), loc.at[5])
+
+    def send_dup(k):
+        for i, d in enumerate(dup_list):
+            @pl.when(g != d)
+            def _():
+                dup_copy(i, k, here).start()
 
     for i, d in enumerate(dup_list):
         @pl.when(g == d)
@@ -654,13 +677,13 @@
     pl.semaphore_wait(bar, G + jnp.where(seam, G - 1, 0))
 
     def far_copy(j, sd):
-        return rc(far, ff.at[sd, lax.rem(j, half), lev(lax.div(j, half))], p_s.at[0], p_r.at[0, sd * G + j], end_dev)
+        return rc(far, ff.at[sd, lax.rem(j, half), lev(lax.div(j, half))], p_s.at[0], p_r.at[0], end_dev)
 
     def wt_copy(j, sd):
-        return rc(fw, wts.at[sd, lax.rem(j, half), lev(lax.div(j, half))], p_s.at[1], p_r.at[1, sd * G + j], mix_dev)
+        return rc(fw, wts.at[sd, lax.rem(j, half), lev(lax.div(j, half))], p_s.at[1], p_r.at[1], mix_dev)
 
     def ix_copy(j, sd):
-        return rc(fidx, fi.at[sd, lax.rem(j, half), lax.div(j, half)], p_s.at[2], p_r.at[2, sd * G + j], mix_dev)
+        return rc(fidx, fi.at[sd, lax.rem(j, half), lax.div(j, half)], p_s.at[2], p_r.at[2], mix_dev)
 
     own_far = pltpu.make_async_copy(far, ff.at[side, place, lev(me)], loc.at[1])
     own_wt = pltpu.make_async_copy(fw, wts.at[side, place, lev(me)], loc.at[2])
@@ -683,50 +706,32 @@
     def _():
         wt_copy(here, side).start()
         ix_copy(here, side).start()
-
-    parts = ((0, reach), (reach, R - reach))
 
     def in_copy(i, j, src):
         lo, n = parts[i]
         return rc(state.at[:, :, pl.ds(slab_of(j) * R + lo, n)],
                   q.at[0, lax.rem(src, half), lev(lax.div(src, half)), :, pl.ds(lo, n)],
-                  in_s.at[i, j], in_r.at[i, src], dev(j, side))
-
-    @pl.loop(0, G - 1)
-    def _(t):
-        in_copy(0, peer(t), here).start()
-
-    for i, d in enumerate(dup_list):
-        @pl.when(g != d)
-        def _():
-            dup_copy(i, here).start()
-
-    @pl.loop(0, G - 1)
-    def _(t):
-        in_copy(1, peer(t), here).start()
+                  in_s.at[i], in_r.at[i], dev(j, side))
+
+    def send_in(i):
+        @pl.loop(0, G - 1)
+        def _(t):
+            in_copy(i, peer(t), here).start()
+
+    send_in(0)
+    send_dup(0)
+    send_in(1)
+    send_dup(1)
 
     lane = lax.broadcasted_iota(jnp.int32, (8, 128), 1)
     sub = lax.broadcasted_iota(jnp.int32, (8, 128), 0)
     first_lane, last_lane = lane == 0, lane == 127
 
-    def others(sd):
-        def each(body):
-            @pl.loop(0, G - 1)
-            def _(t):
-                body(peer(t), sd)
-
-            @pl.loop(0, G)
-            def _(j):
-                body(j, 1 - sd)
-        return each
-
     @pl.when(ends)
     def _():
         own_far.wait()
 
-        @others(1)
-        def _(j, sd):
-            far_copy(j, sd).wait_recv()
+        received(q.at[0, :, pl.ds(0, L // half), :, pl.ds(0, 2 * G - 1)], p_r.at[0])
 
         for k in range(2):
             for b in range(half):
@@ -740,10 +745,8 @@
         own_wt.wait()
         own_ix.wait()
 
-        @others(0)
-        def _(j, sd):
-            wt_copy(j, sd).wait_recv()
-            ix_copy(j, sd).wait_recv()
+        received(q.at[0, :, pl.ds(0, L // half), :, pl.ds(0, 2 * G - 1)], p_r.at[1])
+        received(q.at[0, 0, 0, pl.ds(0, L), pl.ds(0, 2 * G - 1)], p_r.at[2])
 
         for r in range(2):
             for b in range(half):
@@ -772,8 +775,18 @@
     own_speed = speeds(side)
     next_speed = speeds(next_side)
 
-    def feed():
-        return rc(q.at[0, :, :, :, pl.ds(0, reach)], q.at[0, :, :, :, pl.ds(R, reach)], h_s.at[0], h_r.at[0], prev_dev)
+    def feed(k):
+        lo, n = ahead[k]
+        return rc(q.at[0, :, :, :, pl.ds(lo, n)], q.at[0, :, :, :, pl.ds(R + lo, n)], h_s.at[k], h_r.at[k], prev_dev)
+
+    def wait_ahead(k):
+        @pl.when(takes_dup)
+        def _():
+            received(gather_of(ahead[k][1]), dup_r.at[k])
+
+        @pl.when(jnp.logical_not(takes_dup))
+        def _():
+            feed(k).wait_recv()
 
     def time_pass(s, w):
         c = SECTION_FACTORS[s - 1]
@@ -788,7 +801,9 @@
                 for l in range(NT):
                     tt[b, l, v] = (q[0, b, l, v, at] + terms[l]) - (4.0 * DISSIPATION * c) * xs[l]
 
-    def space_pass(s, w, lo, hi, ghosts=False, border=False):
+    def space_pass(s, w, lo, hi):
+        up_row, dn_row = w + lo <= R - 1 < w + hi, w + lo <= R < w + hi
+        border = w + hi > R
         c = SECTION_FACTORS[s - 1]
         hh = 0.5 * c
         near = DISSIPATION * c
@@ -801,9 +816,8 @@
             beyond = sub >= R - w
             cu, cd, cr, cl = [jnp.where(beyond, n, o) for n, o in zip(weights(next_speed), (cu, cd, cr, cl))]
         span = range(half)
-        if ghosts:
-            up_at = sub == jnp.where(seam, R - 1 - w, 8)
-            dn_at = sub == jnp.where(seam, R - w, 8)
+        up_at = sub == jnp.where(seam, R - 1 - w, 8)
+        dn_at = sub == jnp.where(seam, R - w, 8)
 
         def level(l):
             di = [[None] * half for _ in range(4)]
@@ -816,9 +830,10 @@
                 for b in span:
                     up = q[s - 1, b, l, v, pl.ds(w + 1, 8)]
                     dn = q[s - 1, b, l, v, pl.ds(w - 1, 8)]
-                    if ghosts:
-                        at = pl.ds(4 * l + v, 1)
+                    at = pl.ds(4 * l + v, 1)
+                    if up_row:
                         up = jnp.where(up_at, jnp.broadcast_to(gg[0, b, at], (8, 128)), up)
+                    if dn_row:
                         dn = jnp.where(dn_at, jnp.broadcast_to(gg[1, b, at], (8, 128)), dn)
                     right = jnp.where(last_lane, rr[(b + 1) % half], rr[b])
                     left = jnp.where(first_lane, rl[(b - 1) % half], rl[b])
@@ -832,8 +847,8 @@
                 new = [acc[0][b] - cross, acc[1][b] - hh * di[3][b], acc[2][b] - hh * dj[3][b], acc[3][b] - cross]
                 for v in range(4):
                     q[s, b, l, v, pl.ds(w + lo, hi - lo)] = new[v][lo:hi]
-                    if ghosts and s < nsec:
-                        for k in range(2):
+                    for k, hit in enumerate((up_row, dn_row)):
+                        if hit and s < nsec:
                             row = R - 1 + k - w
                             fo[k, b, pl.ds(4 * l + v, 1)] = new[v][row:row + 1]
 
@@ -844,36 +859,21 @@
 
     own.wait()
 
-    @pl.loop(0, G - 1)
-    def _(t):
-        j = peer(G - 2 - t)
-        in_copy(0, j, j).wait_recv()
+    received(gather_of(parts[0][1]), in_r.at[0])
 
     @pl.when(feeds_prev)
     def _():
-        feed().start()
-
-    for s in range(1, 4):
-        w = min(s, reach - 8)
-        time_pass(s, w)
-        space_pass(s, w, s - w, reach - s - w)
-
-    @pl.loop(0, G - 1)
-    def _(t):
-        j = peer(G - 2 - t)
-        in_copy(1, j, j).wait_recv()
-
-    for s in range(1, nsec + 1):
-        if s < 4:
-            w = R - 8 - s
-            lo, hi = reach - s - w, 8
-        else:
-            w = (R - 8) // 2
-            lo, hi = s - w, R - s - w
-        time_pass(s, w)
-        space_pass(s, w, lo, hi)
-
-    spans = ((nsec, R - 2 * nsec), (R - nsec, nsec), (R, nsec))
+        feed(0).start()
+        feed(1).start()
+
+    early = first - reach
+    following = lax.rem(g + 1, G)
+    takes_own = jnp.logical_not(seam)
+    turn = nsec + early + 8
+    spans = [(nsec, early), (nsec + early, 8), (turn, R - turn), (R, nsec)]
+    spans = [(lo, n) for lo, n in spans if n > 0]
+    last = len(spans) - 1
+    inner = 1 if early else 0
 
     def result(i, j):
         lo, n = spans[i]
@@ -881,37 +881,43 @@
 
     def spot(i, gs):
         lo, n = spans[i]
-        return out.at[:, :, pl.ds(gs * R + (lo if i < 2 else 0), n)]
+        return out.at[:, :, pl.ds(gs * R + (lo if i < last else 0), n)]
 
     def out_copy(i, j, gs):
-        return rc(result(i, j), spot(i, gs), out_s.at[i, j], out_r.at[i, gs], dev(j, side if i < 2 else next_side))
+        return rc(result(i, j), spot(i, gs), out_s.at[i], out_r.at[i], dev(j, side if i < last else next_side))
 
     def own_out(i, gs):
-        return pltpu.make_async_copy(result(i, here), spot(i, gs), loc.at[5 + i])
-
-    following = lax.rem(g + 1, G)
-    takes_own = jnp.logical_not(seam)
-
-    @pl.loop(0, G - 1)
-    def _(t):
-        out_copy(0, peer(t), g).start()
+        return pltpu.make_async_copy(result(i, here), spot(i, gs), loc.at[6 + i])
+
+    def send_out(i):
+        @pl.loop(0, G - 1)
+        def _(t):
+            out_copy(i, peer(t), g).start()
+
+        own_out(i, g).start()
+
+    def window(s, w, lo, hi):
+        time_pass(s, w)
+        space_pass(s, w, lo - w, hi - w)
+
+    for s in range(1, nsec + 1):
+        lo, hi = s, first - s
+        if hi - lo > 8:
+            window(s, lo, lo, lo + 8)
+            window(s, hi - 8, lo + 8, hi)
+        elif hi > lo:
+            window(s, min(lo, first - 8 - (s == 1)), lo, hi)
+    if early:
+        send_out(0)
+
+    received(gather_of(parts[1][1]), in_r.at[1])
 
     for i, d in enumerate(dup_list):
         @pl.when(g == d)
         def _():
             own_dup(i).wait()
 
-    @pl.when(takes_dup)
-    def _():
-        @pl.loop(0, G - 1)
-        def _(t):
-            dup_copy(0, peer(t)).wait_recv()
-
-    @pl.when(jnp.logical_not(takes_dup))
-    def _():
-        feed().wait_recv()
-
-    own_out(0, g).start()
+    wait_ahead(0)
 
     @pl.when(mixes)
     def _():
@@ -922,7 +928,7 @@
                     for k in range(2):
                         fo[k, b, pl.ds(4 * l + v, 1)] = q[0, b, l, v, pl.ds(R - 1 + k, 1)]
 
-    for s in range(1, nsec + 1):
+    def mix():
         @pl.when(mixes)
         def _():
             @pl.loop(0, groups)
@@ -939,61 +945,48 @@
                             total = total + ww[r, k, b, at] * picked
                         gg[r, b, at] = total
 
-        time_pass(s, R - s)
-        space_pass(s, R - s, 0, 8, True, True)
-        time_pass(s, R + 2 - s)
-        space_pass(s, R + 2 - s, 6, 8, False, True)
+    for s in range(1, nsec + 1):
+        if s <= first - 8:
+            mix()
+        window(s, first - s, first - s, first - s + 8)
+    send_out(inner)
+    wait_ahead(1)
+
+    for s in range(1, nsec + 1):
+        if s > first - 8:
+            mix()
+        window(s, R + 2 - s, first + 8 - s, R + reach - s)
 
     @pl.loop(0, G - 1)
     def _(t):
-        out_copy(1, peer(t), g).start()
-        out_copy(2, peer(t), following).start()
-
-    own_out(1, g).start()
+        for i in range(inner + 1, last):
+            out_copy(i, peer(t), g).start()
+        out_copy(last, peer(t), following).start()
+
+    for i in range(inner + 1, last):
+        own_out(i, g).start()
 
     @pl.when(takes_own)
     def _():
-        own_out(2, following).start()
+        own_out(last, following).start()
 
     @pl.when(seam)
     def _():
-        out_copy(2, here, following).start()
-
-    @pl.loop(0, G - 1)
-    def _(t):
-        gs = lax.rem(g + 1 + t, G)
-        out_copy(0, here, gs).wait_recv()
-        out_copy(1, here, gs).wait_recv()
-        out_copy(2, here, lax.rem(gs + 1, G)).wait_recv()
-
-    @pl.when(takes_own)
-    def _():
-        own_out(2, following).wait()
-
-    @pl.when(seam)
-    def _():
-        out_copy(2, here, following).wait_recv()
-        out_copy(2, here, following).wait_send()
-
-    own_out(0, g).wait()
-    own_out(1, g).wait()
-
-    @pl.loop(0, G - 1)
-    def _(t):
-        j = peer(t)
-        in_copy(0, j, here).wait_send()
-        in_copy(1, j, here).wait_send()
-        for i in range(3):
-            out_copy(i, j, g).wait_send()
+        out_copy(last, here, following).start()
+
+    for i in range(2):
+        sent(gather_of(parts[i][1]), in_s.at[i])
 
     for i, d in enumerate(dup_list):
         @pl.when(g != d)
         def _():
-            dup_copy(i, here).wait_send()
+            for k in range(2):
+                dup_copy(i, k, here).wait_send()
 
     @pl.when(feeds_prev)
     def _():
-        feed().wait_send()
+        feed(0).wait_send()
+        feed(1).wait_send()
 
     @pl.when(jnp.logical_not(ends))
     def _():
@@ -1003,6 +996,22 @@
     def _():
         wt_copy(here, side).wait_send()
         ix_copy(here, side).wait_send()
+
+    for i in range(last):
+        own_out(i, g).wait()
+        sent(gather_of(spans[i][1]), out_s.at[i])
+        received(gather_of(spans[i][1]), out_r.at[i])
+
+    @pl.when(takes_own)
+    def _():
+        own_out(last, following).wait()
+        sent(gather_of(nsec), out_s.at[last])
+        received(gather_of(nsec), out_r.at[last])
+
+    @pl.when(seam)
+    def _():
+        sent(gather_of(nsec, True), out_s.at[last])
+        received(gather_of(nsec, True), out_r.at[last])
 
 
 def ring_shards(dims, state, far_field, face_index, face_weight, mean_flow):
@@ -1036,12 +1045,12 @@
             V((2, half, 4 * NT, width), f32),
             V((2, half, 4 * NT, width), f32),
             pltpu.SMEM((2, 2), f32),
-            dma((2, G)), dma((2, G)),
-            dma((tm_n,)), dma((G,)),
-            dma((3, G)), dma((3, G)),
-            dma((3,)), dma((3, 2 * G)),
-            dma((1,)), dma((1,)),
-            dma((8,)),
+            dma((2,)), dma((2,)),
+            dma((tm_n // 2 - 2, 2)), dma((2,)),
+            dma((4,)), dma((4,)),
+            dma((3,)), dma((3,)),
+            dma((2,)), dma((2,)),
+            dma((10,)),
         ],
         compiler_params=pltpu.CompilerParams(
             collective_id=0, has_side_effects=True, vmem_limit_bytes=48 * 1024 * 1024),
@@ -1061,8 +1070,8 @@
 
     def body(state, *rest):
         tm_n, half = dims
-        fits = (half == 2 and tm_n % 2 == 0 and tm_n >= 4 and state.shape[2] == 16 * tm_n * half
-                and state.shape[3] == 128 and state.shape[0] * tm_n % 8 == 0)
+        fits = (half == 2 and tm_n in (6, 8) and state.shape[0] % 2 == 0 and state.shape[0] * tm_n % 8 == 0
+                and rest[2].shape[1] == 4 and state.shape[2] == 16 * tm_n * half and state.shape[3] == 128)
         return (ring_shards if fits else shards)(dims, state, *rest)
 
     return jax.shard_map(body, mesh=mesh, in_specs=in_specs, out_specs=out_specs, check_vma=False)

time: 61.6 us -> 57.9 us (0.940)
  Pallas kernels: 60.5 us -> 56.6 us
    pallas_call x1, Pallas kernels: 60.5 us -> 56.6 us  [ring_shards(): pl.pallas_call(functools.partial(ring_kernel, (tm_n, half, L, R, K)), out...]
where the time goes in v3:
time: 57.9 us; the launch traced here: 57.6 us
  Pallas kernels  56.6 us (98%)
  local copies, waits for them, and re-layouts  0.97 us (2%)
    pallas_call x1, Pallas kernels, ring_shards(): pl.pallas_call(functools.partial(ring_kernel, (tm_n, half, L, R, K)), out...  56.6 us

profile of v3, /device:TPU:25, one launch (start us, length us, event | category | flops | bytes accessed | tf_op | source)
XLA Modules:
  0.0 57.6 jit_solution(15289304015781354064)
XLA Ops:
  0.0 56.6 %shard_map.55 = f32[2,4,256,128]{3,2,1,0:T(8,128)S(1)} custom-call(f32[2,4,256,128]{3,2,1,0:T(8,128)} %state.1, f32[2,4,128]{2,1,0:T(4,128)} %far.1, s32[2,128]{1,0:T(2,128)} %fidx.1, f32[2,4,128]{2,1,0:T(4,128)} %fw.1, f32[2,2]{1,0:T(2,128)} %mf.1), custom_call_target="tpu_custom_call" | custom-call | tf_op jit(solution)/shard_map/pallas_call | solution.py:1031
  56.7 1.0 %copy.7 = f32[2,4,256,128]{3,2,1,0:T(8,128)} copy(f32[2,4,256,128]{3,2,1,0:T(8,128)S(1)} %shard_map.55) | data formatting | bytes 2097152

commit v4 on v3

--- a/solution.py
+++ b/solution.py
@@ -12,7 +12,7 @@
 OMEGA = 1.0
 DISSIPATION = 0.2
 PAD = 8
-FIRST_ROWS = 11
+FIRST_ROWS = 13
 MESH = pl.DeviceIdType.MESH
 
 
@@ -543,8 +543,8 @@
     return [ev[n] + od[n] for n in range(half)] + [ev[n] - od[n] for n in range(half)]
 
 
-def ring_kernel(dims, state, far, fidx, fw, mf, out, q, tt, ff, wts, fi, lane_ix, blk_ix, ww, gg, fo, mfs,
-                in_s, in_r, dup_s, dup_r, out_s, out_r, p_s, p_r, h_s, h_r, loc):
+def ring_kernel(dims, state, far, fidx, fw, mf, out, q, tt, dd, ff, wts, fi, lane_ix, blk_ix, ww, gg, fo, mfs,
+                info, in_s, in_r, dup_s, dup_r, out_s, out_r, p_s, p_r, h_s, h_r, loc):
     tm_n, half, L, R, K = dims
     NT = tm_n * L
     G = tm_n * half
@@ -614,7 +614,7 @@
                                             device_id=to, device_id_type=MESH)
 
     def gather_of(n, whole=False):
-        return q.at[0, :, pl.ds(0, NT if whole else NT - L // half), :, pl.ds(0, n)]
+        return q[0].at[:, pl.ds(0, NT if whole else NT - L // half), :, pl.ds(0, n)]
 
     def received(view, sem):
         rc(view, view, p_s.at[0], sem, end_dev).wait_recv()
@@ -622,30 +622,29 @@
     def sent(view, sem):
         rc(view, view, sem, p_r.at[0], end_dev).wait_send()
 
+    z = lax.div(me, 2)
+
+    def near(j):
+        return jnp.abs(lax.div(lax.div(j, half), 2) - z) <= 1
+
+    partner = {"block": (1 - side) * half + place}
     bar = pltpu.get_barrier_semaphore()
 
     @pl.loop(0, G - 1)
     def _(t):
-        pl.semaphore_signal(bar, inc=1, device_id=dev(peer(t), side), device_id_type=MESH)
-
-    @pl.when(seam)
-    def _():
-        @pl.loop(0, G)
-        def _(j):
-            pl.semaphore_signal(bar, inc=1, device_id=dev(j, 1 - side), device_id_type=MESH)
-
-    @pl.when(jnp.logical_not(seam))
-    def _():
-        pl.semaphore_signal(bar, inc=1, device_id=device(G - 1, 1 - side), device_id_type=MESH)
+        @pl.when(near(peer(t)))
+        def _():
+            pl.semaphore_signal(bar, inc=1, device_id=dev(peer(t), side), device_id_type=MESH)
+
+    pl.semaphore_signal(bar, inc=1, device_id=partner, device_id_type=MESH)
 
     own = pltpu.make_async_copy(state.at[:, :, pl.ds(pl.multiple_of(g * R, R), R)],
-                                q.at[0, place, lev(me), :, pl.ds(0, R)], loc.at[0])
+                                q[0].at[place, lev(me), :, pl.ds(0, R)], loc.at[0])
     own.start()
     own_mf = pltpu.make_async_copy(mf, mfs, loc.at[4])
     own_mf.start()
 
     first = FIRST_ROWS
-    parts = ((0, first), (first, R - first))
     ahead = ((0, first - 8), (first - 8, reach + 8 - first), (0, reach))
 
     def ahead_rows(d, k):
@@ -654,7 +653,7 @@
 
     def ahead_spot(j, k):
         lo, n = ahead[k]
-        return q.at[0, lax.rem(j, half), lev(lax.div(j, half)), :, pl.ds(R + lo, n)]
+        return q[0].at[lax.rem(j, half), lev(lax.div(j, half)), :, pl.ds(R + lo, n)]
 
     def dup_copy(i, k, j):
         return rc(ahead_rows(dup_list[i], k), ahead_spot(j, k), dup_s.at[i, k], dup_r.at[k],
@@ -674,7 +673,48 @@
         def _():
             own_dup(i).start()
 
-    pl.semaphore_wait(bar, G + jnp.where(seam, G - 1, 0))
+    pl.semaphore_wait(bar, 2 * half * (1 + jnp.where(z > 0, 1, 0) + jnp.where(z < Z - 1, 1, 0)))
+
+    parts = ((0, first), (first, R - first))
+
+    def in_copy(i, j, src):
+        lo, n = parts[i]
+        return rc(state.at[:, :, pl.ds(slab_of(j) * R + lo, n)],
+                  q[0].at[lax.rem(src, half), lev(lax.div(src, half)), :, pl.ds(lo, n)],
+                  in_s.at[i], in_r.at[i], dev(j, side))
+
+    def send_in(i, which=None):
+        @pl.loop(0, G - 1)
+        def _(t):
+            if which is None:
+                in_copy(i, peer(t), here).start()
+            else:
+                @pl.when(near(peer(t)) == which)
+                def _():
+                    in_copy(i, peer(t), here).start()
+
+    send_in(0, True)
+
+    for r in range(1, Z - 1):
+        @pl.when((z >= 1) & (z + r <= Z - 1))
+        def _():
+            pl.semaphore_signal(info.at[r], inc=1, device_id={"tm": me - 2}, device_id_type=MESH)
+
+        @pl.when((z <= Z - 2) & (z - r >= 0))
+        def _():
+            pl.semaphore_signal(info.at[Z + r], inc=1, device_id={"tm": me + 2}, device_id_type=MESH)
+
+        @pl.when(z + r + 1 <= Z - 1)
+        def _():
+            pl.semaphore_wait(info.at[r], 1)
+
+        @pl.when(z - r - 1 >= 0)
+        def _():
+            pl.semaphore_wait(info.at[Z + r], 1)
+
+    send_in(0, False)
+    pl.semaphore_signal(info.at[0], inc=1, device_id=partner, device_id_type=MESH)
+    pl.semaphore_wait(info.at[0], 1)
 
     def far_copy(j, sd):
         return rc(far, ff.at[sd, lax.rem(j, half), lev(lax.div(j, half))], p_s.at[0], p_r.at[0], end_dev)
@@ -707,18 +747,6 @@
         wt_copy(here, side).start()
         ix_copy(here, side).start()
 
-    def in_copy(i, j, src):
-        lo, n = parts[i]
-        return rc(state.at[:, :, pl.ds(slab_of(j) * R + lo, n)],
-                  q.at[0, lax.rem(src, half), lev(lax.div(src, half)), :, pl.ds(lo, n)],
-                  in_s.at[i], in_r.at[i], dev(j, side))
-
-    def send_in(i):
-        @pl.loop(0, G - 1)
-        def _(t):
-            in_copy(i, peer(t), here).start()
-
-    send_in(0)
     send_dup(0)
     send_in(1)
     send_dup(1)
@@ -731,7 +759,7 @@
     def _():
         own_far.wait()
 
-        received(q.at[0, :, pl.ds(0, L // half), :, pl.ds(0, 2 * G - 1)], p_r.at[0])
+        received(q[0].at[:, pl.ds(0, L // half), :, pl.ds(0, 2 * G - 1)], p_r.at[0])
 
         for k in range(2):
             for b in range(half):
@@ -745,8 +773,8 @@
         own_wt.wait()
         own_ix.wait()
 
-        received(q.at[0, :, pl.ds(0, L // half), :, pl.ds(0, 2 * G - 1)], p_r.at[1])
-        received(q.at[0, 0, 0, pl.ds(0, L), pl.ds(0, 2 * G - 1)], p_r.at[2])
+        received(q[0].at[:, pl.ds(0, L // half), :, pl.ds(0, 2 * G - 1)], p_r.at[1])
+        received(q[0].at[0, 0, pl.ds(0, L), pl.ds(0, 2 * G - 1)], p_r.at[2])
 
         for r in range(2):
             for b in range(half):
@@ -777,7 +805,7 @@
 
     def feed(k):
         lo, n = ahead[k]
-        return rc(q.at[0, :, :, :, pl.ds(lo, n)], q.at[0, :, :, :, pl.ds(R + lo, n)], h_s.at[k], h_r.at[k], prev_dev)
+        return rc(q[0].at[:, :, :, pl.ds(lo, n)], q[0].at[:, :, :, pl.ds(R + lo, n)], h_s.at[k], h_r.at[k], prev_dev)
 
     def wait_ahead(k):
         @pl.when(takes_dup)
@@ -788,74 +816,66 @@
         def _():
             feed(k).wait_recv()
 
-    def time_pass(s, w):
+    span = range(half)
+
+    def window(s, w, lo, hi):
+        old, new = q[s - 1], q[s]
         c = SECTION_FACTORS[s - 1]
         even, odd = split_coefficients(NT, -OMEGA * c)
         at = pl.ds(w, 8)
+        up_row, dn_row = lo <= R - 1 < hi, lo <= R < hi
+        hh = 0.5 * c
+        near = DISSIPATION * c
+
+        def weights(uv):
+            return near - hh * uv[0], near + hh * uv[0], near - hh * uv[1], near + hh * uv[1]
+
+        cu, cd, cr, cl = weights(own_speed)
+        if hi > R:
+            beyond = sub >= R - w
+            cu, cd, cr, cl = [jnp.where(beyond, n, o) for n, o in zip(weights(next_speed), (cu, cd, cr, cl))]
+        up_at = sub == jnp.where(seam, R - 1 - w, 8)
+        dn_at = sub == jnp.where(seam, R - w, 8)
 
         @pl.loop(0, 4)
         def _(v):
-            for b in range(half):
-                xs = [q[s - 1, b, l, v, at] for l in range(NT)]
+            for b in span:
+                xs = [old[b, l, v, at] for l in range(NT)]
                 terms = time_term_split(xs, even, odd)
                 for l in range(NT):
-                    tt[b, l, v] = (q[0, b, l, v, at] + terms[l]) - (4.0 * DISSIPATION * c) * xs[l]
-
-    def space_pass(s, w, lo, hi):
-        up_row, dn_row = w + lo <= R - 1 < w + hi, w + lo <= R < w + hi
-        border = w + hi > R
-        c = SECTION_FACTORS[s - 1]
-        hh = 0.5 * c
-        near = DISSIPATION * c
-
-        def weights(uv):
-            return near - hh * uv[0], near + hh * uv[0], near - hh * uv[1], near + hh * uv[1]
-
-        cu, cd, cr, cl = weights(own_speed)
-        if border:
-            beyond = sub >= R - w
-            cu, cd, cr, cl = [jnp.where(beyond, n, o) for n, o in zip(weights(next_speed), (cu, cd, cr, cl))]
-        span = range(half)
-        up_at = sub == jnp.where(seam, R - 1 - w, 8)
-        dn_at = sub == jnp.where(seam, R - w, 8)
-
-        def level(l):
-            di = [[None] * half for _ in range(4)]
-            dj = [[None] * half for _ in range(4)]
-            acc = [[None] * half for _ in range(4)]
-            for v in range(4):
-                x = [q[s - 1, b, l, v, pl.ds(w, 8)] for b in span]
+                    tt[b, l, v] = (q[0][b, l, v, at] + terms[l]) - (4.0 * DISSIPATION * c) * xs[l]
+            for l in range(NT):
+                x = [old[b, l, v, at] for b in span]
                 rr = [pltpu.roll(x[b], 127, 1) for b in span]
                 rl = [pltpu.roll(x[b], 1, 1) for b in span]
                 for b in span:
-                    up = q[s - 1, b, l, v, pl.ds(w + 1, 8)]
-                    dn = q[s - 1, b, l, v, pl.ds(w - 1, 8)]
-                    at = pl.ds(4 * l + v, 1)
+                    up = old[b, l, v, pl.ds(w + 1, 8)]
+                    dn = old[b, l, v, pl.ds(w - 1, 8)]
+                    row = pl.ds(4 * l + v, 1)
                     if up_row:
-                        up = jnp.where(up_at, jnp.broadcast_to(gg[0, b, at], (8, 128)), up)
+                        up = jnp.where(up_at, jnp.broadcast_to(gg[0, b, row], (8, 128)), up)
                     if dn_row:
-                        dn = jnp.where(dn_at, jnp.broadcast_to(gg[1, b, at], (8, 128)), dn)
+                        dn = jnp.where(dn_at, jnp.broadcast_to(gg[1, b, row], (8, 128)), dn)
                     right = jnp.where(last_lane, rr[(b + 1) % half], rr[b])
                     left = jnp.where(first_lane, rl[(b - 1) % half], rl[b])
-                    acc[v][b] = (tt[b, l, v] + (cu * up + cd * dn)) + (cr * right + cl * left)
-                    if v in (1, 3):
-                        di[v][b] = up - dn
-                    if v in (2, 3):
-                        dj[v][b] = right - left
-            for b in span:
-                cross = hh * (di[1][b] + dj[2][b])
-                new = [acc[0][b] - cross, acc[1][b] - hh * di[3][b], acc[2][b] - hh * dj[3][b], acc[3][b] - cross]
-                for v in range(4):
-                    q[s, b, l, v, pl.ds(w + lo, hi - lo)] = new[v][lo:hi]
-                    for k, hit in enumerate((up_row, dn_row)):
-                        if hit and s < nsec:
-                            row = R - 1 + k - w
-                            fo[k, b, pl.ds(4 * l + v, 1)] = new[v][row:row + 1]
+                    tt[b, l, v] = (tt[b, l, v] + (cu * up + cd * dn)) + (cr * right + cl * left)
+                    dd[0, b, l, v] = hh * (up - dn)
+                    dd[1, b, l, v] = hh * (right - left)
 
         @pl.loop(0, NT // 4)
         def _(i):
             for j in range(4):
-                level(4 * i + j)
+                l = 4 * i + j
+                for b in span:
+                    cross = dd[0, b, l, 1] + dd[1, b, l, 2]
+                    drop = [cross, dd[0, b, l, 3], dd[1, b, l, 3], cross]
+                    for v in range(4):
+                        value = tt[b, l, v] - drop[v]
+                        new[b, l, v, pl.ds(lo, hi - lo)] = value[lo - w:hi - w]
+                        for k, hit in enumerate((up_row, dn_row)):
+                            if hit and s < nsec:
+                                row = R - 1 + k - w
+                                fo[k, b, pl.ds(4 * l + v, 1)] = value[row:row + 1]
 
     own.wait()
 
@@ -877,7 +897,7 @@
 
     def result(i, j):
         lo, n = spans[i]
-        return q.at[nsec, lax.rem(j, half), lev(lax.div(j, half)), :, pl.ds(lo, n)]
+        return q[nsec].at[lax.rem(j, half), lev(lax.div(j, half)), :, pl.ds(lo, n)]
 
     def spot(i, gs):
         lo, n = spans[i]
@@ -895,10 +915,6 @@
             out_copy(i, peer(t), g).start()
 
         own_out(i, g).start()
-
-    def window(s, w, lo, hi):
-        time_pass(s, w)
-        space_pass(s, w, lo - w, hi - w)
 
     for s in range(1, nsec + 1):
         lo, hi = s, first - s
@@ -926,7 +942,7 @@
             for b in range(half):
                 for v in range(4):
                     for k in range(2):
-                        fo[k, b, pl.ds(4 * l + v, 1)] = q[0, b, l, v, pl.ds(R - 1 + k, 1)]
+                        fo[k, b, pl.ds(4 * l + v, 1)] = q[0][b, l, v, pl.ds(R - 1 + k, 1)]
 
     def mix():
         @pl.when(mixes)
@@ -1034,8 +1050,9 @@
         in_specs=[hbm] * 5,
         out_specs=hbm,
         scratch_shapes=[
-            V((n + 1, half, NT, 4, R + 16, width), f32),
+            [V((half, NT, 4, R + 16, width), f32) for _ in range(n + 1)],
             V((half, NT, 4, 8, width), f32),
+            V((2, half, NT, 4, 8, width), f32),
             V((2, half, NT, 4, width), f32),
             V((2, half, NT, K, width), f32),
             V((2, half, tm_n, L, width), jnp.int32),
@@ -1045,6 +1062,7 @@
             V((2, half, 4 * NT, width), f32),
             V((2, half, 4 * NT, width), f32),
             pltpu.SMEM((2, 2), f32),
+            pltpu.SemaphoreType.REGULAR((tm_n,)),
             dma((2,)), dma((2,)),
             dma((tm_n // 2 - 2, 2)), dma((2,)),
             dma((4,)), dma((4,)),

time: 57.9 us -> 56 us (0.967)
  Pallas kernels: 56.6 us -> 54.8 us
    pallas_call x1, Pallas kernels: 56.6 us -> 54.8 us  [ring_shards(): pl.pallas_call(functools.partial(ring_kernel, (tm_n, half, L, R, K)), out...]
where the time goes in v4:
time: 56 us; the launch traced here: 55.8 us
  Pallas kernels  54.8 us (98%)
  local copies, waits for them, and re-layouts  0.97 us (2%)
    pallas_call x1, Pallas kernels, ring_shards(): pl.pallas_call(functools.partial(ring_kernel, (tm_n, half, L, R, K)), out...  54.8 us

profile of v4, /device:TPU:25, one launch (start us, length us, event | category | flops | bytes accessed | tf_op | source)
XLA Modules:
  0.0 55.8 jit_solution(14661820906438847627)
XLA Ops:
  0.0 54.8 %shard_map.55 = f32[2,4,256,128]{3,2,1,0:T(8,128)S(1)} custom-call(f32[2,4,256,128]{3,2,1,0:T(8,128)} %state.1, f32[2,4,128]{2,1,0:T(4,128)} %far.1, s32[2,128]{1,0:T(2,128)} %fidx.1, f32[2,4,128]{2,1,0:T(4,128)} %fw.1, f32[2,2]{1,0:T(2,128)} %mf.1), custom_call_target="tpu_custom_call" | custom-call | tf_op jit(solution)/shard_map/pallas_call | solution.py:1047
  54.8 1.0 %copy.7 = f32[2,4,256,128]{3,2,1,0:T(8,128)} copy(f32[2,4,256,128]{3,2,1,0:T(8,128)S(1)} %shard_map.55) | data formatting | bytes 2097152

commit v5 on v4

--- a/solution.py
+++ b/solution.py
@@ -748,7 +748,8 @@
         ix_copy(here, side).start()
 
     send_dup(0)
-    send_in(1)
+    send_in(1, True)
+    send_in(1, False)
     send_dup(1)
 
     lane = lax.broadcasted_iota(jnp.int32, (8, 128), 1)

time: 56 us -> 55.6 us (level)
  no operation moved by 1% of the time
where the time goes in v5:
time: 55.6 us; the launch traced here: 55.5 us
  Pallas kernels  54.5 us (98%)
  local copies, waits for them, and re-layouts  0.97 us (2%)
    pallas_call x1, Pallas kernels, ring_shards(): pl.pallas_call(functools.partial(ring_kernel, (tm_n, half, L, R, K)), out...  54.5 us

profile of v5, /device:TPU:25, one launch (start us, length us, event | category | flops | bytes accessed | tf_op | source)
XLA Modules:
  0.0 55.5 jit_solution(9961208348344273242)
XLA Ops:
  0.0 54.5 %shard_map.55 = f32[2,4,256,128]{3,2,1,0:T(8,128)S(1)} custom-call(f32[2,4,256,128]{3,2,1,0:T(8,128)} %state.1, f32[2,4,128]{2,1,0:T(4,128)} %far.1, s32[2,128]{1,0:T(2,128)} %fidx.1, f32[2,4,128]{2,1,0:T(4,128)} %fw.1, f32[2,2]{1,0:T(2,128)} %mf.1), custom_call_target="tpu_custom_call" | custom-call | tf_op jit(solution)/shard_map/pallas_call | solution.py:1048
  54.5 1.0 %copy.7 = f32[2,4,256,128]{3,2,1,0:T(8,128)} copy(f32[2,4,256,128]{3,2,1,0:T(8,128)S(1)} %shard_map.55) | data formatting | bytes 2097152

commit v6 on v5

--- a/solution.py
+++ b/solution.py
@@ -702,7 +702,7 @@
 
         @pl.when((z <= Z - 2) & (z - r >= 0))
         def _():
-            pl.semaphore_signal(info.at[Z + r], inc=1, device_id={"tm": me + 2}, device_id_type=MESH)
+            pl.semaphore_signal(info.at[Z - 2 + r], inc=1, device_id={"tm": me + 2}, device_id_type=MESH)
 
         @pl.when(z + r + 1 <= Z - 1)
         def _():
@@ -710,7 +710,7 @@
 
         @pl.when(z - r - 1 >= 0)
         def _():
-            pl.semaphore_wait(info.at[Z + r], 1)
+            pl.semaphore_wait(info.at[Z - 2 + r], 1)
 
     send_in(0, False)
     pl.semaphore_signal(info.at[0], inc=1, device_id=partner, device_id_type=MESH)
@@ -913,7 +913,7 @@
     def send_out(i):
         @pl.loop(0, G - 1)
         def _(t):
-            out_copy(i, peer(t), g).start()
+            out_copy(i, peer(lax.rem(t + 3, G - 1)), g).start()
 
         own_out(i, g).start()
 
@@ -1063,7 +1063,7 @@
             V((2, half, 4 * NT, width), f32),
             V((2, half, 4 * NT, width), f32),
             pltpu.SMEM((2, 2), f32),
-            pltpu.SemaphoreType.REGULAR((tm_n,)),
+            pltpu.SemaphoreType.REGULAR((tm_n - 3,)),
             dma((2,)), dma((2,)),
             dma((tm_n // 2 - 2, 2)), dma((2,)),
             dma((4,)), dma((4,)),

time: 55.6 us -> 55.4 us (level)
  no operation moved by 1% of the time
where the time goes in v6:
time: 55.4 us; the launch traced here: 55.3 us
  Pallas kernels  54.3 us (98%)
  local copies, waits for them, and re-layouts  0.97 us (2%)
    pallas_call x1, Pallas kernels, ring_shards(): pl.pallas_call(functools.partial(ring_kernel, (tm_n, half, L, R, K)), out...  54.3 us

profile of v6, /device:TPU:25, one launch (start us, length us, event | category | flops | bytes accessed | tf_op | source)
XLA Modules:
  0.0 55.3 jit_solution(10427897796700101947)
XLA Ops:
  0.0 54.3 %shard_map.55 = f32[2,4,256,128]{3,2,1,0:T(8,128)S(1)} custom-call(f32[2,4,256,128]{3,2,1,0:T(8,128)} %state.1, f32[2,4,128]{2,1,0:T(4,128)} %far.1, s32[2,128]{1,0:T(2,128)} %fidx.1, f32[2,4,128]{2,1,0:T(4,128)} %fw.1, f32[2,2]{1,0:T(2,128)} %mf.1), custom_call_target="tpu_custom_call" | custom-call | tf_op jit(solution)/shard_map/pallas_call | solution.py:1048
  54.3 1.0 %copy.7 = f32[2,4,256,128]{3,2,1,0:T(8,128)} copy(f32[2,4,256,128]{3,2,1,0:T(8,128)S(1)} %shard_map.55) | data formatting | bytes 2097152
